TPU v7x, 256 devices: a 4x2x16 block of a 4x16x16 slice. The times are simulated.
256 devices in a mesh: parts: 2 (over y), gz: 32 (over z, core), shot: 4 (over x).
Axes of the slice: x: 4, y: 2, z: 16, core: 2. Of those that a mesh axis runs over, the one named last changes fastest.
The devices are a block of a 4x16x16 slice.
Arguments:
- wavefields: float32 [8, 2, 9, 128, 32, 128], P(('parts', 'shot'), None, None, 'gz'), parts along dimension 0, may hold values from -6 to 6
- earth_model: float32 [6, 128, 32, 128], P('parts', 'gz'), parts along dimension 0, may hold values from 0.4 to 1.6
- source_depth: int32 [8], P(('parts', 'shot')), parts along dimension 0, may hold values from 0 to 127
- source_column: int32 [8], P(('parts', 'shot')), parts along dimension 0, may hold values from 0 to 4095
- wavelet: float32 [8, 8], P(('parts', 'shot')), parts along dimension 0, may hold values from -30 to 30
- receiver_depth: int32 [8, 64], P(('parts', 'shot')), parts along dimension 0, may hold values from 0 to 127
- receiver_column: int32 [8, 64], P(('parts', 'shot')), parts along dimension 0, may hold values from 0 to 4095
- traces: float32 [8, 8, 64], P(('parts', 'shot')), parts along dimension 0, may hold values from -30 to 30
Outputs:
- images: float32 [4, 128, 32, 128], P('parts', 'gz'), parts along dimension 0
There are 2 independent parts, one for each index of `parts`. A program takes and returns all parts, laid end to end along the dimension named above; each array names one. Nothing has to cross between parts.
All inputs are finite; a program needn't handle non-finite values.
Results may differ from a plain program's by a relative error of at most 0.00002.
Values sent between devices are 32-bit elements; how exact they have to be, the bound alone decides.
A program may use at most 64 MiB of HBM per device.

v0:
```python
import jax
import jax.numpy as jnp
from jax import lax
from jax.sharding import PartitionSpec as P

time_step = 0.15


def shifted(value, axis, steps):
    count = lax.axis_size(axis)
    first, last = (max(0, -steps), min(count, count - steps))
    return lax.ppermute(value, axis, [(source, source + steps) for source in range(first, last)])


def copy_for_each(value, axis):
    size = lax.axis_size(axis)
    return lax.all_to_all(
        jnp.broadcast_to(value[None], (size, *value.shape)), axis, 0, 0, tiled=True
    )


def of_everyone(value, axis):
    everything = copy_for_each(value, axis)
    return jnp.sum(everything, axis=0)


def together(arrays, axis):
    line, at, outs = (jnp.concatenate([a.reshape(-1) for a in arrays]), 0, [])
    total = of_everyone(line, axis)
    for a in arrays:
        outs.append(total[at : at + a.size].reshape(a.shape))
        at += a.size
    return tuple(outs)


def forward_diff(array, dim_index):
    length = array.shape[dim_index]
    following = jnp.concatenate(
        [
            lax.slice_in_dim(array, 1, length, axis=dim_index),
            jnp.zeros_like(lax.slice_in_dim(array, 0, 1, axis=dim_index)),
        ],
        axis=dim_index,
    )
    return following - array


def backward_diff(array, dim_index):
    length = array.shape[dim_index]
    previous = jnp.concatenate(
        [
            jnp.zeros_like(lax.slice_in_dim(array, 0, 1, axis=dim_index)),
            lax.slice_in_dim(array, 0, length - 1, axis=dim_index),
        ],
        axis=dim_index,
    )
    return array - previous


def depth_forward(array, plane_high):
    following = jnp.concatenate([array[:, 1:], plane_high[:, None]], axis=1)
    return following - array


def depth_backward(array, plane_low):
    previous = jnp.concatenate([plane_low[:, None], array[:, :-1]], axis=1)
    return array - previous


def velocity_half(fields, buoyancy, sxz_low, syz_low, szz_high):
    vel_x, vel_y, vel_z, sig_xx, sig_yy, sig_zz, sig_xy, sig_xz, sig_yz = fields
    vel_x = vel_x + time_step * buoyancy * (
        forward_diff(sig_xx, 2) + backward_diff(sig_xy, 3) + depth_backward(sig_xz, sxz_low)
    )
    vel_y = vel_y + time_step * buoyancy * (
        backward_diff(sig_xy, 2) + forward_diff(sig_yy, 3) + depth_backward(sig_yz, syz_low)
    )
    vel_z = vel_z + time_step * buoyancy * (
        backward_diff(sig_xz, 2) + backward_diff(sig_yz, 3) + depth_forward(sig_zz, szz_high)
    )
    return (vel_x, vel_y, vel_z)


def stress_half(fields, lame_lambda, shear_mu, vz_low, vx_high, vy_high):
    vel_x, vel_y, vel_z, sig_xx, sig_yy, sig_zz, sig_xy, sig_xz, sig_yz = fields
    strain_x = backward_diff(vel_x, 2)
    strain_y = backward_diff(vel_y, 3)
    strain_z = depth_backward(vel_z, vz_low)
    spread = strain_x + strain_y + strain_z
    sig_xx = sig_xx + time_step * (lame_lambda * spread + 2.0 * shear_mu * strain_x)
    sig_yy = sig_yy + time_step * (lame_lambda * spread + 2.0 * shear_mu * strain_y)
    sig_zz = sig_zz + time_step * (lame_lambda * spread + 2.0 * shear_mu * strain_z)
    vx_up = depth_forward(vel_x, vx_high)
    vy_up = depth_forward(vel_y, vy_high)
    vz_along_x = forward_diff(vel_z, 2)
    vz_along_y = forward_diff(vel_z, 3)
    vx_along_y = forward_diff(vel_x, 3)
    vy_along_x = forward_diff(vel_y, 2)
    sig_xy = sig_xy + time_step * shear_mu * (vx_along_y + vy_along_x)
    sig_xz = sig_xz + time_step * shear_mu * (vx_up + vz_along_x)
    sig_yz = sig_yz + time_step * shear_mu * (vy_up + vz_along_y)
    rotation = vz_along_y - vy_up + (vx_up - vz_along_x) + (vy_along_x - vx_along_y)
    return ([vel_x, vel_y, vel_z, sig_xx, sig_yy, sig_zz, sig_xy, sig_xz, sig_yz], rotation)


def add_points(field_in, wave_index, depth_at, row_index, col_index, amounts, limit_at):
    inside = (depth_at >= 0) & (depth_at < limit_at)
    place_at = jnp.where(inside, depth_at, limit_at)
    return field_in.at[wave_index, place_at, row_index, col_index].add(amounts, mode="drop")


def advance(fields, material, receiver_add, source_add):
    stress_lows = shifted(jnp.stack([fields[7][:, -1], fields[8][:, -1]]), "gz", 1)
    sxz_low = stress_lows[0]
    syz_low = stress_lows[1]
    szz_high = shifted(fields[5][:, 0], "gz", -1)
    vel_x, vel_y, vel_z = velocity_half(fields, material[0], sxz_low, syz_low, szz_high)
    vel_z = receiver_add(vel_z)
    vz_low = shifted(vel_z[:, -1], "gz", 1)
    vel_highs = shifted(jnp.stack([vel_x[:, 0], vel_y[:, 0]]), "gz", -1)
    vx_high = vel_highs[0]
    vy_high = vel_highs[1]
    updated, rotation = stress_half(
        [vel_x, vel_y, vel_z] + list(fields[3:]), material[1], material[2], vz_low, vx_high, vy_high
    )
    for field_no in (3, 4, 5):
        updated[field_no] = source_add(updated[field_no])
    return (updated, rotation)


def on_device(
    wavefields,
    earth_model,
    source_depth,
    source_column,
    wavelet,
    receiver_depth,
    receiver_column,
    traces,
):
    fields_now = wavefields[0]
    slab_depth = fields_now.shape[2]
    width_y = fields_now.shape[4]
    steps_total = wavelet.shape[1]
    offset = lax.axis_index("gz") * slab_depth
    src_row = source_column[0] // width_y
    src_col = source_column[0] % width_y
    rec_row = receiver_column[0] // width_y
    rec_col = receiver_column[0] % width_y
    tallies = {
        "image_pp": jnp.zeros(fields_now.shape[2:], jnp.float32),
        "image_ps": jnp.zeros(fields_now.shape[2:], jnp.float32),
        "first_half": None,
    }

    def tally(step_index, pressure, rotation):
        tallies["image_pp"] = tallies["image_pp"] + pressure[0] * pressure[1]
        tallies["image_ps"] = tallies["image_ps"] + pressure[0] * rotation[1]
        if step_index == steps_total // 2 - 1:
            tallies["first_half"] = together((tallies["image_pp"], tallies["image_ps"]), "shot")
            tallies["image_pp"] = jnp.zeros_like(tallies["image_pp"])
            tallies["image_ps"] = jnp.zeros_like(tallies["image_ps"])

    def injectors(step_index, limit_at):

        def receiver_add(vel_z):
            return add_points(
                vel_z,
                1,
                receiver_depth[0] - offset,
                rec_row,
                rec_col,
                time_step * traces[0, step_index],
                limit_at,
            )

        def source_add(normal):
            return add_points(
                normal,
                0,
                source_depth[0] - offset,
                src_row,
                src_col,
                time_step * wavelet[0, step_index],
                limit_at,
            )

        return (receiver_add, source_add)

    fields = [fields_now[:, field_no] for field_no in range(9)]
    for step_index in range(steps_total):
        receiver_add, source_add = injectors(step_index, slab_depth)
        fields, rotation = advance(fields, earth_model, receiver_add, source_add)
        pressure = (fields[3] + fields[4] + fields[5]) / 3.0
        tally(step_index, pressure, rotation)
    summed_pp, summed_ps = together((tallies["image_pp"], tallies["image_ps"]), "shot")
    summed_pp = summed_pp + tallies["first_half"][0]
    summed_ps = summed_ps + tallies["first_half"][1]
    return jnp.stack([summed_pp, summed_ps]) / steps_total


def solution(mesh):
    placed = (
        P(("parts", "shot"), None, None, "gz", None, None),
        P("parts", "gz", None, None),
        P(("parts", "shot")),
        P(("parts", "shot")),
        P(("parts", "shot"), None),
        P(("parts", "shot"), None),
        P(("parts", "shot"), None),
        P(("parts", "shot"), None, None),
    )
    return jax.shard_map(
        on_device,
        mesh=mesh,
        in_specs=placed,
        out_specs=P("parts", "gz", None, None),
        check_vma=False,
    )
```

profile of v0, /device:TPU:33, one launch (start us, length us, event | category | flops | bytes accessed | tf_op | source)
XLA Modules:
  0.0 278.0 jit_solution(14094540140864914330)
XLA Ops:
  0.0 1.4 copy.935
  1.6 5.7 %collective-permute-start = (f32[2,2,32,128]{3,2,1,0:T(8,128)S(1)}, f32[2,2,32,128]{3,2,1,0:T(8,128)S(1)}, u32[]{:S(2)}, u32[]{:S(2)}) collective-permute-start(f32[2,2,32,128]{3,2,1,0:T(8,128)S(1)} %pad_maximum_fusion.4), channel_id=1, source_target_pairs={{0,4},{4,8},{8,12},{12,16},{16,20},{20,24},{24,28},{28,32},{32,36}... | collective-permute-start | bytes 196616 | tf_op jit(solution)/shard_map/ppermute | solution.py:12
  7.3 17.9 %collective-permute-start.1 = (f32[2,32,128]{2,1,0:T(8,128)S(1)}, f32[2,32,128]{2,1,0:T(8,128)S(1)}, u32[]{:S(2)}, u32[]{:S(2)}) collective-permute-start(f32[2,32,128]{2,1,0:T(8,128)S(1)} %slice_bitcast_fusion.85), channel_id=1, source_target_pairs={{4,0},{8,4},{12,8},{16,12},{20,16},{24,20},{28,24},{32,28},{36,32}... | collective-permute-start | bytes 98312 | tf_op jit(solution)/shard_map/ppermute | solution.py:12
  33.7 2.0 collective-permute-start.3
  35.7 5.3 %scatter_fusion = f32[2,4,32,128]{3,2,1,0:T(8,128)S(1)} fusion(f32[2,4,32,128]{3,2,1,0:T(8,128)S(1)} %copy.495, s32[64]{0:T(128)S(1)} %fusion.123, f32[64]{0:T(128)S(1)} %get-tuple-element.513), kind=kCustom, calls=%fused_computation | custom fusion | flops 64 | bytes 1792 | tf_op jit(solution)/shard_map/scatter-add | solution.py:109
  41.3 3.7 %collective-permute-start.2 = (f32[2,32,128]{2,1,0:T(8,128)S(1)}, f32[2,32,128]{2,1,0:T(8,128)S(1)}, u32[]{:S(2)}, u32[]{:S(2)}) collective-permute-start(f32[2,32,128]{2,1,0:T(8,128)S(1)} %slice_bitcast_fusion.84), channel_id=1, source_target_pairs={{0,4},{4,8},{8,12},{12,16},{16,20},{20,24},{24,28},{28,32},{32,36}... | collective-permute-start | bytes 98312 | tf_op jit(solution)/shard_map/ppermute | solution.py:12
  47.1 4.3 %collective-permute-start.4 = (f32[2,2,32,128]{3,2,1,0:T(8,128)S(1)}, f32[2,2,32,128]{3,2,1,0:T(8,128)S(1)}, u32[]{:S(2)}, u32[]{:S(2)}) collective-permute-start(f32[2,2,32,128]{3,2,1,0:T(8,128)S(1)} %pad_maximum_fusion.6), channel_id=1, source_target_pairs={{0,4},{4,8},{8,12},{12,16},{16,20},{20,24},{24,28},{28,32},{32,36}... | collective-permute-start | bytes 196616 | tf_op jit(solution)/shard_map/ppermute | solution.py:12
  59.3 2.0 collective-permute-start.5
  61.6 2.0 collective-permute-start.7
  64.7 5.3 %scatter_fusion.1 = f32[2,4,32,128]{3,2,1,0:T(8,128)S(1)} fusion(f32[2,4,32,128]{3,2,1,0:T(8,128)S(1)} %get-tuple-element.468, s32[64]{0:T(128)S(1)} %fusion.123, f32[64]{0:T(128)S(1)} %get-tuple-element.512), kind=kCustom, calls=%fused_computation.1 | custom fusion | flops 64 | bytes 1792 | tf_op jit(solution)/shard_map/scatter-add | solution.py:109
  70.3 2.7 collective-permute-start.6
  78.6 2.0 collective-permute-start.9
  83.4 4.3 %collective-permute-start.8 = (f32[2,2,32,128]{3,2,1,0:T(8,128)S(1)}, f32[2,2,32,128]{3,2,1,0:T(8,128)S(1)}, u32[]{:S(2)}, u32[]{:S(2)}) collective-permute-start(f32[2,2,32,128]{3,2,1,0:T(8,128)S(1)} %pad_maximum_fusion.8), channel_id=1, source_target_pairs={{0,4},{4,8},{8,12},{12,16},{16,20},{20,24},{24,28},{28,32},{32,36}... | collective-permute-start | bytes 196616 | tf_op jit(solution)/shard_map/ppermute | solution.py:12
  90.6 5.3 %scatter_fusion.2 = f32[2,4,32,128]{3,2,1,0:T(8,128)S(1)} fusion(f32[2,4,32,128]{3,2,1,0:T(8,128)S(1)} %copy.539, s32[64]{0:T(128)S(1)} %fusion.123, f32[64]{0:T(128)S(1)} %get-tuple-element.511), kind=kCustom, calls=%fused_computation.2 | custom fusion | flops 64 | bytes 1792 | tf_op jit(solution)/shard_map/scatter-add | solution.py:109
  96.1 2.4 collective-permute-start.10
  99.5 2.0 collective-permute-start.11
  106.1 3.4 %collective-permute-start.12 = (f32[2,2,32,128]{3,2,1,0:T(8,128)S(1)}, f32[2,2,32,128]{3,2,1,0:T(8,128)S(1)}, u32[]{:S(2)}, u32[]{:S(2)}) collective-permute-start(f32[2,2,32,128]{3,2,1,0:T(8,128)S(1)} %pad_maximum_fusion.10), channel_id=1, source_target_pairs={{0,4},{4,8},{8,12},{12,16},{16,20},{20,24},{24,28},{28,32},{32,36}... | collective-permute-start | bytes 196616 | tf_op jit(solution)/shard_map/ppermute | solution.py:12
  114.9 2.0 collective-permute-start.13
  117.1 3.1 %collective-permute-done.13 = f32[2,32,128]{2,1,0:T(8,128)S(1)} collective-permute-done((f32[2,32,128]{2,1,0:T(8,128)S(1)}, f32[2,32,128]{2,1,0:T(8,128)S(1)}, u32[]{:S(2)}, u32[]{:S(2)}) %collective-permute-start.13) | collective-permute-done | bytes 32800 | tf_op jit(solution)/shard_map/ppermute | solution.py:12
  120.6 2.1 collective-permute-start.15
  122.7 5.3 %scatter_fusion.3 = f32[2,4,32,128]{3,2,1,0:T(8,128)S(1)} fusion(f32[2,4,32,128]{3,2,1,0:T(8,128)S(1)} %copy.572, s32[64]{0:T(128)S(1)} %fusion.123, f32[64]{0:T(128)S(1)} %get-tuple-element.510), kind=kCustom, calls=%fused_computation.3 | custom fusion | flops 64 | bytes 1792 | tf_op jit(solution)/shard_map/scatter-add | solution.py:109
  128.4 3.7 %collective-permute-start.14 = (f32[2,32,128]{2,1,0:T(8,128)S(1)}, f32[2,32,128]{2,1,0:T(8,128)S(1)}, u32[]{:S(2)}, u32[]{:S(2)}) collective-permute-start(f32[2,32,128]{2,1,0:T(8,128)S(1)} %slice_bitcast_fusion.54), channel_id=1, source_target_pairs={{0,4},{4,8},{8,12},{12,16},{16,20},{20,24},{24,28},{28,32},{32,36}... | collective-permute-start | bytes 98312 | tf_op jit(solution)/shard_map/ppermute | solution.py:12
  134.1 4.3 %collective-permute-start.16 = (f32[2,2,32,128]{3,2,1,0:T(8,128)S(1)}, f32[2,2,32,128]{3,2,1,0:T(8,128)S(1)}, u32[]{:S(2)}, u32[]{:S(2)}) collective-permute-start(f32[2,2,32,128]{3,2,1,0:T(8,128)S(1)} %pad_maximum_fusion.12), channel_id=1, source_target_pairs={{0,4},{4,8},{8,12},{12,16},{16,20},{20,24},{24,28},{28,32},{32,36}... | collective-permute-start | bytes 196616 | tf_op jit(solution)/shard_map/ppermute | solution.py:12
  141.8 2.0 collective-permute-start.17
  149.4 5.3 %scatter_fusion.4 = f32[2,4,32,128]{3,2,1,0:T(8,128)S(1)} fusion(f32[2,4,32,128]{3,2,1,0:T(8,128)S(1)} %copy.608, s32[64]{0:T(128)S(1)} %fusion.123, f32[64]{0:T(128)S(1)} %get-tuple-element.509), kind=kCustom, calls=%fused_computation.4 | custom fusion | flops 64 | bytes 1792 | tf_op jit(solution)/shard_map/scatter-add | solution.py:109
  155.0 2.0 collective-permute-start.19
  157.1 3.7 %collective-permute-start.18 = (f32[2,32,128]{2,1,0:T(8,128)S(1)}, f32[2,32,128]{2,1,0:T(8,128)S(1)}, u32[]{:S(2)}, u32[]{:S(2)}) collective-permute-start(f32[2,32,128]{2,1,0:T(8,128)S(1)} %slice_bitcast_fusion.44), channel_id=1, source_target_pairs={{0,4},{4,8},{8,12},{12,16},{16,20},{20,24},{24,28},{28,32},{32,36}... | collective-permute-start | bytes 98312 | tf_op jit(solution)/shard_map/ppermute | solution.py:12
  165.2 1.1 broadcast_in_dim.71
  166.3 3.6 %all-to-all-start.1 = ((f32[4,1,32768]{2,1,0:T(1,128)}), f32[4,1,32768]{2,1,0:T(1,128)S(1)}, u32[]{:S(2)}, u32[]{:S(2)}) async-start(f32[4,1,32768]{2,1,0:T(1,128)} %broadcast_in_dim.71), calls=%async_computation.1 | async-start | bytes 1048576 | tf_op jit(solution)/shard_map/all_to_all | solution.py:17
  172.4 4.3 %collective-permute-start.20 = (f32[2,2,32,128]{3,2,1,0:T(8,128)S(1)}, f32[2,2,32,128]{3,2,1,0:T(8,128)S(1)}, u32[]{:S(2)}, u32[]{:S(2)}) collective-permute-start(f32[2,2,32,128]{3,2,1,0:T(8,128)S(1)} %pad_maximum_fusion.14), channel_id=1, source_target_pairs={{0,4},{4,8},{8,12},{12,16},{16,20},{20,24},{24,28},{28,32},{32,36}... | collective-permute-start | bytes 196616 | tf_op jit(solution)/shard_map/ppermute | solution.py:12
  176.7 2.0 collective-permute-start.21
  184.0 5.3 %scatter_fusion.5 = f32[2,4,32,128]{3,2,1,0:T(8,128)S(1)} fusion(f32[2,4,32,128]{3,2,1,0:T(8,128)S(1)} %copy.642, s32[64]{0:T(128)S(1)} %fusion.123, f32[64]{0:T(128)S(1)} %get-tuple-element.508), kind=kCustom, calls=%fused_computation.5 | custom fusion | flops 64 | bytes 1792 | tf_op jit(solution)/shard_map/scatter-add | solution.py:109
  189.6 2.0 collective-permute-start.23
  191.7 3.7 %collective-permute-start.22 = (f32[2,32,128]{2,1,0:T(8,128)S(1)}, f32[2,32,128]{2,1,0:T(8,128)S(1)}, u32[]{:S(2)}, u32[]{:S(2)}) collective-permute-start(f32[2,32,128]{2,1,0:T(8,128)S(1)} %slice_bitcast_fusion.34), channel_id=1, source_target_pairs={{0,4},{4,8},{8,12},{12,16},{16,20},{20,24},{24,28},{28,32},{32,36}... | collective-permute-start | bytes 98312 | tf_op jit(solution)/shard_map/ppermute | solution.py:12
  201.0 4.3 %collective-permute-start.24 = (f32[2,2,32,128]{3,2,1,0:T(8,128)S(1)}, f32[2,2,32,128]{3,2,1,0:T(8,128)S(1)}, u32[]{:S(2)}, u32[]{:S(2)}) collective-permute-start(f32[2,2,32,128]{3,2,1,0:T(8,128)S(1)} %pad_maximum_fusion.16), channel_id=1, source_target_pairs={{0,4},{4,8},{8,12},{12,16},{16,20},{20,24},{24,28},{28,32},{32,36}... | collective-permute-start | bytes 196616 | tf_op jit(solution)/shard_map/ppermute | solution.py:12
  205.3 2.0 collective-permute-start.25
  212.9 5.3 %scatter_fusion.6 = f32[2,4,32,128]{3,2,1,0:T(8,128)S(1)} fusion(f32[2,4,32,128]{3,2,1,0:T(8,128)S(1)} %copy.679, s32[64]{0:T(128)S(1)} %fusion.123, f32[64]{0:T(128)S(1)} %get-tuple-element.514), kind=kCustom, calls=%fused_computation.6 | custom fusion | flops 64 | bytes 1792 | tf_op jit(solution)/shard_map/scatter-add | solution.py:109
  218.3 3.7 %collective-permute-start.26 = (f32[2,32,128]{2,1,0:T(8,128)S(1)}, f32[2,32,128]{2,1,0:T(8,128)S(1)}, u32[]{:S(2)}, u32[]{:S(2)}) collective-permute-start(f32[2,32,128]{2,1,0:T(8,128)S(1)} %slice_bitcast_fusion.24), channel_id=1, source_target_pairs={{0,4},{4,8},{8,12},{12,16},{16,20},{20,24},{24,28},{28,32},{32,36}... | collective-permute-start | bytes 98312 | tf_op jit(solution)/shard_map/ppermute | solution.py:12
  222.9 2.2 collective-permute-start.27
  228.5 1.9 collective-permute-start.29
  232.4 3.7 %collective-permute-start.28 = (f32[2,2,32,128]{3,2,1,0:T(8,128)S(1)}, f32[2,2,32,128]{3,2,1,0:T(8,128)S(1)}, u32[]{:S(2)}, u32[]{:S(2)}) collective-permute-start(f32[2,2,32,128]{3,2,1,0:T(8,128)S(1)} %pad_maximum_fusion.18), channel_id=1, source_target_pairs={{0,4},{4,8},{8,12},{12,16},{16,20},{20,24},{24,28},{28,32},{32,36}... | collective-permute-start | bytes 196616 | tf_op jit(solution)/shard_map/ppermute | solution.py:12
  241.9 5.3 %scatter_fusion.7 = f32[2,4,32,128]{3,2,1,0:T(8,128)S(1)} fusion(f32[2,4,32,128]{3,2,1,0:T(8,128)S(1)} %get-tuple-element.413, s32[64]{0:T(128)S(1)} %fusion.123, f32[64]{0:T(128)S(1)} %get-tuple-element.507), kind=kCustom, calls=%fused_computation.7 | custom fusion | flops 64 | bytes 1792 | tf_op jit(solution)/shard_map/scatter-add | solution.py:109
  247.2 2.4 collective-permute-start.30
  249.9 2.0 collective-permute-start.31
  260.2 1.4 fusion.98
  261.7 1.1 broadcast_in_dim.70
  262.7 4.1 %all-to-all-start = ((f32[4,1,32768]{2,1,0:T(1,128)}), f32[4,1,32768]{2,1,0:T(1,128)S(1)}, u32[]{:S(2)}, u32[]{:S(2)}) async-start(f32[4,1,32768]{2,1,0:T(1,128)} %broadcast_in_dim.70), calls=%async_computation | async-start | bytes 1048576 | tf_op jit(solution)/shard_map/all_to_all | solution.py:17
  267.4 9.4 %all-to-all-done = f32[4,1,32768]{2,1,0:T(1,128)S(1)} async-done(((f32[4,1,32768]{2,1,0:T(1,128)}), f32[4,1,32768]{2,1,0:T(1,128)S(1)}, u32[]{:S(2)}, u32[]{:S(2)}) %all-to-all-start) | async-done | bytes 524320 | tf_op jit(solution)/shard_map/all_to_all | solution.py:17
  (404 shorter events, 49.6 us)
Async XLA Ops:
  1.4 25.2 %copy-start.24 = (f32[3,4,32,128]{3,2,1,0:T(8,128)S(1)}, f32[3,4,32,128]{3,2,1,0:T(8,128)}, u32[]{:S(2)}) copy-start(f32[3,4,32,128]{3,2,1,0:T(8,128)} %param.57) | copy-start | bytes 589828
  1.5 25.3 %copy-start.26 = (f32[1,8,64]{2,1,0:T(8,128)S(1)}, f32[1,8,64]{2,1,0:T(8,128)}, u32[]{:S(2)}) copy-start(f32[1,8,64]{2,1,0:T(8,128)} %param.63) | copy-start | bytes 6148
  1.5 25.4 %copy-start.25 = (f32[1,8]{1,0:T(1,128)S(1)}, f32[1,8]{1,0:T(1,128)}, u32[]{:S(2)}) copy-start(f32[1,8]{1,0:T(1,128)} %param.60) | copy-start | bytes 100
  1.5 31.0 %copy-start.27 = (s32[1,64]{1,0:T(1,128)S(1)}, s32[1,64]{1,0:T(1,128)}, u32[]{:S(2)}) copy-start(s32[1,64]{1,0:T(1,128)} %param.62) | copy-start | bytes 772
  1.5 31.0 %copy-start.28 = (s32[1,64]{1,0:T(1,128)S(1)}, s32[1,64]{1,0:T(1,128)}, u32[]{:S(2)}) copy-start(s32[1,64]{1,0:T(1,128)} %param.61) | copy-start | bytes 772
  1.5 31.1 %copy-start.29 = (s32[4]{0:T(128)S(1)}, s32[4]{0:T(128)}, u32[]{:S(2)}) copy-start(s32[4]{0:T(128)} %constant.524.clone.1) | copy-start | bytes 52
  1.6 31.7 %collective-permute-start = (f32[2,2,32,128]{3,2,1,0:T(8,128)S(1)}, f32[2,2,32,128]{3,2,1,0:T(8,128)S(1)}, u32[]{:S(2)}, u32[]{:S(2)}) collective-permute-start(f32[2,2,32,128]{3,2,1,0:T(8,128)S(1)} %pad_maximum_fusion.4), channel_id=1, source_target_pairs={{0,4},{4,8},{8,12},{12,16},{16,20},{20,24},{24,28},{28,32},{32,36}... | collective-permute-start | bytes 196616 | tf_op jit(solution)/shard_map/ppermute | solution.py:12
  7.3 26.0 %collective-permute-start.1 = (f32[2,32,128]{2,1,0:T(8,128)S(1)}, f32[2,32,128]{2,1,0:T(8,128)S(1)}, u32[]{:S(2)}, u32[]{:S(2)}) collective-permute-start(f32[2,32,128]{2,1,0:T(8,128)S(1)} %slice_bitcast_fusion.85), channel_id=1, source_target_pairs={{4,0},{8,4},{12,8},{16,12},{20,16},{24,20},{28,24},{32,28},{36,32}... | collective-permute-start | bytes 98312 | tf_op jit(solution)/shard_map/ppermute | solution.py:12
  33.7 11.3 %collective-permute-start.3 = (f32[2,2,32,128]{3,2,1,0:T(8,128)S(1)}, f32[2,2,32,128]{3,2,1,0:T(8,128)S(1)}, u32[]{:S(2)}, u32[]{:S(2)}) collective-permute-start(f32[2,2,32,128]{3,2,1,0:T(8,128)S(1)} %pad_maximum_fusion.5), channel_id=1, source_target_pairs={{4,0},{8,4},{12,8},{16,12},{20,16},{24,20},{28,24},{32,28},{36,32}... | collective-permute-start | bytes 196616 | tf_op jit(solution)/shard_map/ppermute | solution.py:12
  41.3 4.7 %collective-permute-start.2 = (f32[2,32,128]{2,1,0:T(8,128)S(1)}, f32[2,32,128]{2,1,0:T(8,128)S(1)}, u32[]{:S(2)}, u32[]{:S(2)}) collective-permute-start(f32[2,32,128]{2,1,0:T(8,128)S(1)} %slice_bitcast_fusion.84), channel_id=1, source_target_pairs={{0,4},{4,8},{8,12},{12,16},{16,20},{20,24},{24,28},{28,32},{32,36}... | collective-permute-start | bytes 98312 | tf_op jit(solution)/shard_map/ppermute | solution.py:12
  47.1 14.2 %collective-permute-start.4 = (f32[2,2,32,128]{3,2,1,0:T(8,128)S(1)}, f32[2,2,32,128]{3,2,1,0:T(8,128)S(1)}, u32[]{:S(2)}, u32[]{:S(2)}) collective-permute-start(f32[2,2,32,128]{3,2,1,0:T(8,128)S(1)} %pad_maximum_fusion.6), channel_id=1, source_target_pairs={{0,4},{4,8},{8,12},{12,16},{16,20},{20,24},{24,28},{28,32},{32,36}... | collective-permute-start | bytes 196616 | tf_op jit(solution)/shard_map/ppermute | solution.py:12
  59.3 5.3 %collective-permute-start.5 = (f32[2,32,128]{2,1,0:T(8,128)S(1)}, f32[2,32,128]{2,1,0:T(8,128)S(1)}, u32[]{:S(2)}, u32[]{:S(2)}) collective-permute-start(f32[2,32,128]{2,1,0:T(8,128)S(1)} %slice_bitcast_fusion.75), channel_id=1, source_target_pairs={{4,0},{8,4},{12,8},{16,12},{20,16},{24,20},{28,24},{32,28},{36,32}... | collective-permute-start | bytes 98312 | tf_op jit(solution)/shard_map/ppermute | solution.py:12
  61.6 11.4 %collective-permute-start.7 = (f32[2,2,32,128]{3,2,1,0:T(8,128)S(1)}, f32[2,2,32,128]{3,2,1,0:T(8,128)S(1)}, u32[]{:S(2)}, u32[]{:S(2)}) collective-permute-start(f32[2,2,32,128]{3,2,1,0:T(8,128)S(1)} %pad_maximum_fusion.7), channel_id=1, source_target_pairs={{4,0},{8,4},{12,8},{16,12},{20,16},{24,20},{28,24},{32,28},{36,32}... | collective-permute-start | bytes 196616 | tf_op jit(solution)/shard_map/ppermute | solution.py:12
  70.3 3.7 %collective-permute-start.6 = (f32[2,32,128]{2,1,0:T(8,128)S(1)}, f32[2,32,128]{2,1,0:T(8,128)S(1)}, u32[]{:S(2)}, u32[]{:S(2)}) collective-permute-start(f32[2,32,128]{2,1,0:T(8,128)S(1)} %slice_bitcast_fusion.74), channel_id=1, source_target_pairs={{0,4},{4,8},{8,12},{12,16},{16,20},{20,24},{24,28},{28,32},{32,36}... | collective-permute-start | bytes 98312 | tf_op jit(solution)/shard_map/ppermute | solution.py:12
  78.6 11.9 %collective-permute-start.9 = (f32[2,32,128]{2,1,0:T(8,128)S(1)}, f32[2,32,128]{2,1,0:T(8,128)S(1)}, u32[]{:S(2)}, u32[]{:S(2)}) collective-permute-start(f32[2,32,128]{2,1,0:T(8,128)S(1)} %slice_bitcast_fusion.65), channel_id=1, source_target_pairs={{4,0},{8,4},{12,8},{16,12},{20,16},{24,20},{28,24},{32,28},{36,32}... | collective-permute-start | bytes 98312 | tf_op jit(solution)/shard_map/ppermute | solution.py:12
  83.4 15.2 %collective-permute-start.8 = (f32[2,2,32,128]{3,2,1,0:T(8,128)S(1)}, f32[2,2,32,128]{3,2,1,0:T(8,128)S(1)}, u32[]{:S(2)}, u32[]{:S(2)}) collective-permute-start(f32[2,2,32,128]{3,2,1,0:T(8,128)S(1)} %pad_maximum_fusion.8), channel_id=1, source_target_pairs={{0,4},{4,8},{8,12},{12,16},{16,20},{20,24},{24,28},{28,32},{32,36}... | collective-permute-start | bytes 196616 | tf_op jit(solution)/shard_map/ppermute | solution.py:12
  96.1 5.4 %collective-permute-start.10 = (f32[2,32,128]{2,1,0:T(8,128)S(1)}, f32[2,32,128]{2,1,0:T(8,128)S(1)}, u32[]{:S(2)}, u32[]{:S(2)}) collective-permute-start(f32[2,32,128]{2,1,0:T(8,128)S(1)} %slice_bitcast_fusion.64), channel_id=1, source_target_pairs={{0,4},{4,8},{8,12},{12,16},{16,20},{20,24},{24,28},{28,32},{32,36}... | collective-permute-start | bytes 98312 | tf_op jit(solution)/shard_map/ppermute | solution.py:12
  99.5 5.8 %collective-permute-start.11 = (f32[2,2,32,128]{3,2,1,0:T(8,128)}, f32[2,2,32,128]{3,2,1,0:T(8,128)S(1)}, u32[]{:S(2)}, u32[]{:S(2)}) collective-permute-start(f32[2,2,32,128]{3,2,1,0:T(8,128)} %pad_maximum_fusion.9), channel_id=1, source_target_pairs={{4,0},{8,4},{12,8},{16,12},{20,16},{24,20},{28,24},{32,28},{36,32}... | collective-permute-start | bytes 196616 | tf_op jit(solution)/shard_map/ppermute | solution.py:12
  106.1 10.9 %collective-permute-start.12 = (f32[2,2,32,128]{3,2,1,0:T(8,128)S(1)}, f32[2,2,32,128]{3,2,1,0:T(8,128)S(1)}, u32[]{:S(2)}, u32[]{:S(2)}) collective-permute-start(f32[2,2,32,128]{3,2,1,0:T(8,128)S(1)} %pad_maximum_fusion.10), channel_id=1, source_target_pairs={{0,4},{4,8},{8,12},{12,16},{16,20},{20,24},{24,28},{28,32},{32,36}... | collective-permute-start | bytes 196616 | tf_op jit(solution)/shard_map/ppermute | solution.py:12
  114.9 5.3 %collective-permute-start.13 = (f32[2,32,128]{2,1,0:T(8,128)S(1)}, f32[2,32,128]{2,1,0:T(8,128)S(1)}, u32[]{:S(2)}, u32[]{:S(2)}) collective-permute-start(f32[2,32,128]{2,1,0:T(8,128)S(1)} %slice_bitcast_fusion.55), channel_id=1, source_target_pairs={{4,0},{8,4},{12,8},{16,12},{20,16},{24,20},{28,24},{32,28},{36,32}... | collective-permute-start | bytes 98312 | tf_op jit(solution)/shard_map/ppermute | solution.py:12
  120.6 11.5 %collective-permute-start.15 = (f32[2,2,32,128]{3,2,1,0:T(8,128)S(1)}, f32[2,2,32,128]{3,2,1,0:T(8,128)S(1)}, u32[]{:S(2)}, u32[]{:S(2)}) collective-permute-start(f32[2,2,32,128]{3,2,1,0:T(8,128)S(1)} %pad_maximum_fusion.11), channel_id=1, source_target_pairs={{4,0},{8,4},{12,8},{16,12},{20,16},{24,20},{28,24},{32,28},{36,32}... | collective-permute-start | bytes 196616 | tf_op jit(solution)/shard_map/ppermute | solution.py:12
  128.4 4.7 %collective-permute-start.14 = (f32[2,32,128]{2,1,0:T(8,128)S(1)}, f32[2,32,128]{2,1,0:T(8,128)S(1)}, u32[]{:S(2)}, u32[]{:S(2)}) collective-permute-start(f32[2,32,128]{2,1,0:T(8,128)S(1)} %slice_bitcast_fusion.54), channel_id=1, source_target_pairs={{0,4},{4,8},{8,12},{12,16},{16,20},{20,24},{24,28},{28,32},{32,36}... | collective-permute-start | bytes 98312 | tf_op jit(solution)/shard_map/ppermute | solution.py:12
  134.1 20.6 %collective-permute-start.16 = (f32[2,2,32,128]{3,2,1,0:T(8,128)S(1)}, f32[2,2,32,128]{3,2,1,0:T(8,128)S(1)}, u32[]{:S(2)}, u32[]{:S(2)}) collective-permute-start(f32[2,2,32,128]{3,2,1,0:T(8,128)S(1)} %pad_maximum_fusion.12), channel_id=1, source_target_pairs={{0,4},{4,8},{8,12},{12,16},{16,20},{20,24},{24,28},{28,32},{32,36}... | collective-permute-start | bytes 196616 | tf_op jit(solution)/shard_map/ppermute | solution.py:12
  141.8 7.4 %collective-permute-start.17 = (f32[2,32,128]{2,1,0:T(8,128)S(1)}, f32[2,32,128]{2,1,0:T(8,128)S(1)}, u32[]{:S(2)}, u32[]{:S(2)}) collective-permute-start(f32[2,32,128]{2,1,0:T(8,128)S(1)} %slice_bitcast_fusion.45), channel_id=1, source_target_pairs={{4,0},{8,4},{12,8},{16,12},{20,16},{24,20},{28,24},{32,28},{36,32}... | collective-permute-start | bytes 98312 | tf_op jit(solution)/shard_map/ppermute | solution.py:12
  155.0 6.0 %collective-permute-start.19 = (f32[2,2,32,128]{3,2,1,0:T(8,128)S(1)}, f32[2,2,32,128]{3,2,1,0:T(8,128)S(1)}, u32[]{:S(2)}, u32[]{:S(2)}) collective-permute-start(f32[2,2,32,128]{3,2,1,0:T(8,128)S(1)} %pad_maximum_fusion.13), channel_id=1, source_target_pairs={{4,0},{8,4},{12,8},{16,12},{20,16},{24,20},{28,24},{32,28},{36,32}... | collective-permute-start | bytes 196616 | tf_op jit(solution)/shard_map/ppermute | solution.py:12
  157.1 4.7 %collective-permute-start.18 = (f32[2,32,128]{2,1,0:T(8,128)S(1)}, f32[2,32,128]{2,1,0:T(8,128)S(1)}, u32[]{:S(2)}, u32[]{:S(2)}) collective-permute-start(f32[2,32,128]{2,1,0:T(8,128)S(1)} %slice_bitcast_fusion.44), channel_id=1, source_target_pairs={{0,4},{4,8},{8,12},{12,16},{16,20},{20,24},{24,28},{28,32},{32,36}... | collective-permute-start | bytes 98312 | tf_op jit(solution)/shard_map/ppermute | solution.py:12
  166.3 95.4 %all-to-all-start.1 = ((f32[4,1,32768]{2,1,0:T(1,128)}), f32[4,1,32768]{2,1,0:T(1,128)S(1)}, u32[]{:S(2)}, u32[]{:S(2)}) async-start(f32[4,1,32768]{2,1,0:T(1,128)} %broadcast_in_dim.71), calls=%async_computation.1 | async-start | bytes 1048576 | tf_op jit(solution)/shard_map/all_to_all | solution.py:17
  172.4 16.9 %collective-permute-start.20 = (f32[2,2,32,128]{3,2,1,0:T(8,128)S(1)}, f32[2,2,32,128]{3,2,1,0:T(8,128)S(1)}, u32[]{:S(2)}, u32[]{:S(2)}) collective-permute-start(f32[2,2,32,128]{3,2,1,0:T(8,128)S(1)} %pad_maximum_fusion.14), channel_id=1, source_target_pairs={{0,4},{4,8},{8,12},{12,16},{16,20},{20,24},{24,28},{28,32},{32,36}... | collective-permute-start | bytes 196616 | tf_op jit(solution)/shard_map/ppermute | solution.py:12
  176.7 7.2 %collective-permute-start.21 = (f32[2,32,128]{2,1,0:T(8,128)S(1)}, f32[2,32,128]{2,1,0:T(8,128)S(1)}, u32[]{:S(2)}, u32[]{:S(2)}) collective-permute-start(f32[2,32,128]{2,1,0:T(8,128)S(1)} %slice_bitcast_fusion.35), channel_id=1, source_target_pairs={{4,0},{8,4},{12,8},{16,12},{20,16},{24,20},{28,24},{32,28},{36,32}... | collective-permute-start | bytes 98312 | tf_op jit(solution)/shard_map/ppermute | solution.py:12
  189.6 6.0 %collective-permute-start.23 = (f32[2,2,32,128]{3,2,1,0:T(8,128)S(1)}, f32[2,2,32,128]{3,2,1,0:T(8,128)S(1)}, u32[]{:S(2)}, u32[]{:S(2)}) collective-permute-start(f32[2,2,32,128]{3,2,1,0:T(8,128)S(1)} %pad_maximum_fusion.15), channel_id=1, source_target_pairs={{4,0},{8,4},{12,8},{16,12},{20,16},{24,20},{28,24},{32,28},{36,32}... | collective-permute-start | bytes 196616 | tf_op jit(solution)/shard_map/ppermute | solution.py:12
  191.7 4.7 %collective-permute-start.22 = (f32[2,32,128]{2,1,0:T(8,128)S(1)}, f32[2,32,128]{2,1,0:T(8,128)S(1)}, u32[]{:S(2)}, u32[]{:S(2)}) collective-permute-start(f32[2,32,128]{2,1,0:T(8,128)S(1)} %slice_bitcast_fusion.34), channel_id=1, source_target_pairs={{0,4},{4,8},{8,12},{12,16},{16,20},{20,24},{24,28},{28,32},{32,36}... | collective-permute-start | bytes 98312 | tf_op jit(solution)/shard_map/ppermute | solution.py:12
  201.0 11.7 %collective-permute-start.24 = (f32[2,2,32,128]{3,2,1,0:T(8,128)S(1)}, f32[2,2,32,128]{3,2,1,0:T(8,128)S(1)}, u32[]{:S(2)}, u32[]{:S(2)}) collective-permute-start(f32[2,2,32,128]{3,2,1,0:T(8,128)S(1)} %pad_maximum_fusion.16), channel_id=1, source_target_pairs={{0,4},{4,8},{8,12},{12,16},{16,20},{20,24},{24,28},{28,32},{32,36}... | collective-permute-start | bytes 196616 | tf_op jit(solution)/shard_map/ppermute | solution.py:12
  205.3 7.3 %collective-permute-start.25 = (f32[2,32,128]{2,1,0:T(8,128)S(1)}, f32[2,32,128]{2,1,0:T(8,128)S(1)}, u32[]{:S(2)}, u32[]{:S(2)}) collective-permute-start(f32[2,32,128]{2,1,0:T(8,128)S(1)} %slice_bitcast_fusion.25), channel_id=1, source_target_pairs={{4,0},{8,4},{12,8},{16,12},{20,16},{24,20},{28,24},{32,28},{36,32}... | collective-permute-start | bytes 98312 | tf_op jit(solution)/shard_map/ppermute | solution.py:12
  218.3 6.8 %collective-permute-start.26 = (f32[2,32,128]{2,1,0:T(8,128)S(1)}, f32[2,32,128]{2,1,0:T(8,128)S(1)}, u32[]{:S(2)}, u32[]{:S(2)}) collective-permute-start(f32[2,32,128]{2,1,0:T(8,128)S(1)} %slice_bitcast_fusion.24), channel_id=1, source_target_pairs={{0,4},{4,8},{8,12},{12,16},{16,20},{20,24},{24,28},{28,32},{32,36}... | collective-permute-start | bytes 98312 | tf_op jit(solution)/shard_map/ppermute | solution.py:12
  222.9 7.5 %collective-permute-start.27 = (f32[2,2,32,128]{3,2,1,0:T(8,128)}, f32[2,2,32,128]{3,2,1,0:T(8,128)}, u32[]{:S(2)}, u32[]{:S(2)}) collective-permute-start(f32[2,2,32,128]{3,2,1,0:T(8,128)} %pad_maximum_fusion.17), channel_id=1, source_target_pairs={{4,0},{8,4},{12,8},{16,12},{20,16},{24,20},{28,24},{32,28},{36,32}... | collective-permute-start | bytes 196616 | tf_op jit(solution)/shard_map/ppermute | solution.py:12
  225.2 6.1 %copy-start.1 = (f32[2,4,32,128]{3,2,1,0:T(8,128)S(1)}, f32[2,4,32,128]{3,2,1,0:T(8,128)}, u32[]{:S(2)}) copy-start(f32[2,4,32,128]{3,2,1,0:T(8,128)} %copy-done) | copy-start | bytes 393220
  225.3 6.1 %slice-start = ((f32[2,4,32,128]{3,2,1,0:T(8,128)}), f32[2,3,32,128]{3,2,1,0:T(8,128)S(1)}, s32[]{:S(2)}) async-start(f32[2,4,32,128]{3,2,1,0:T(8,128)} %copy-done), calls=%async_computation.2 | async-start | bytes 196608 | tf_op jit(solution)/shard_map/slice | solution.py:61
  228.5 13.1 %collective-permute-start.29 = (f32[2,32,128]{2,1,0:T(8,128)}, f32[2,32,128]{2,1,0:T(8,128)S(1)}, u32[]{:S(2)}, u32[]{:S(2)}) collective-permute-start(f32[2,32,128]{2,1,0:T(8,128)} %slice_bitcast_fusion.15), channel_id=1, source_target_pairs={{4,0},{8,4},{12,8},{16,12},{20,16},{24,20},{28,24},{32,28},{36,32}... | collective-permute-start | bytes 98312 | tf_op jit(solution)/shard_map/ppermute | solution.py:12
  232.4 9.1 %collective-permute-start.28 = (f32[2,2,32,128]{3,2,1,0:T(8,128)S(1)}, f32[2,2,32,128]{3,2,1,0:T(8,128)S(1)}, u32[]{:S(2)}, u32[]{:S(2)}) collective-permute-start(f32[2,2,32,128]{3,2,1,0:T(8,128)S(1)} %pad_maximum_fusion.18), channel_id=1, source_target_pairs={{0,4},{4,8},{8,12},{12,16},{16,20},{20,24},{24,28},{28,32},{32,36}... | collective-permute-start | bytes 196616 | tf_op jit(solution)/shard_map/ppermute | solution.py:12
  247.2 4.7 %collective-permute-start.30 = (f32[2,32,128]{2,1,0:T(8,128)S(1)}, f32[2,32,128]{2,1,0:T(8,128)S(1)}, u32[]{:S(2)}, u32[]{:S(2)}) collective-permute-start(f32[2,32,128]{2,1,0:T(8,128)S(1)} %slice_bitcast_fusion.14), channel_id=1, source_target_pairs={{0,4},{4,8},{8,12},{12,16},{16,20},{20,24},{24,28},{28,32},{32,36}... | collective-permute-start | bytes 98312 | tf_op jit(solution)/shard_map/ppermute | solution.py:12
  249.9 10.2 %collective-permute-start.31 = (f32[2,2,32,128]{3,2,1,0:T(8,128)S(1)}, f32[2,2,32,128]{3,2,1,0:T(8,128)S(1)}, u32[]{:S(2)}, u32[]{:S(2)}) collective-permute-start(f32[2,2,32,128]{3,2,1,0:T(8,128)S(1)} %pad_maximum_fusion.19), channel_id=1, source_target_pairs={{4,0},{8,4},{12,8},{16,12},{20,16},{24,20},{28,24},{32,28},{36,32}... | collective-permute-start | bytes 196616 | tf_op jit(solution)/shard_map/ppermute | solution.py:12
  252.0 8.1 %copy-start.2 = (f32[2,4,32,128]{3,2,0,1:T(8,128)S(1)}, f32[2,4,32,128]{3,2,0,1:T(8,128)}, u32[]{:S(2)}) copy-start(f32[2,4,32,128]{3,2,0,1:T(8,128)} %get-tuple-element.320) | copy-start | bytes 393220
  252.1 8.1 %copy-start.3 = (f32[2,4,32,128]{3,2,0,1:T(8,128)S(1)}, f32[2,4,32,128]{3,2,0,1:T(8,128)}, u32[]{:S(2)}) copy-start(f32[2,4,32,128]{3,2,0,1:T(8,128)} %get-tuple-element.321) | copy-start | bytes 393220
  252.2 8.0 %copy-start.4 = (f32[2,4,32,128]{3,2,0,1:T(8,128)S(1)}, f32[2,4,32,128]{3,2,0,1:T(8,128)}, u32[]{:S(2)}) copy-start(f32[2,4,32,128]{3,2,0,1:T(8,128)} %get-tuple-element.397) | copy-start | bytes 393220
  252.2 8.0 %copy-start.5 = (f32[2,4,32,128]{3,2,0,1:T(8,128)S(1)}, f32[2,4,32,128]{3,2,0,1:T(8,128)}, u32[]{:S(2)}) copy-start(f32[2,4,32,128]{3,2,0,1:T(8,128)} %get-tuple-element.398) | copy-start | bytes 393220
  252.2 8.0 %copy-start.6 = (f32[2,4,32,128]{3,2,0,1:T(8,128)S(1)}, f32[2,4,32,128]{3,2,0,1:T(8,128)}, u32[]{:S(2)}) copy-start(f32[2,4,32,128]{3,2,0,1:T(8,128)} %get-tuple-element.465) | copy-start | bytes 393220
  252.2 8.0 %copy-start.7 = (f32[2,4,32,128]{3,2,0,1:T(8,128)S(1)}, f32[2,4,32,128]{3,2,0,1:T(8,128)}, u32[]{:S(2)}) copy-start(f32[2,4,32,128]{3,2,0,1:T(8,128)} %get-tuple-element.466) | copy-start | bytes 393220
  262.7 14.1 %all-to-all-start = ((f32[4,1,32768]{2,1,0:T(1,128)}), f32[4,1,32768]{2,1,0:T(1,128)S(1)}, u32[]{:S(2)}, u32[]{:S(2)}) async-start(f32[4,1,32768]{2,1,0:T(1,128)} %broadcast_in_dim.70), calls=%async_computation | async-start | bytes 1048576 | tf_op jit(solution)/shard_map/all_to_all | solution.py:17
  (17 other events, 21.3 us)
where the time goes:
time: 282 us; the launch traced here: 278 us
  starting transfers between devices  115 us (41%)
  other arithmetic  74.2 us (26%)
  between operations  53 us (19%)
  waiting for transfers between devices  18.3 us (6%)
  local copies, waits for them, and re-layouts  17.2 us (6%)
    ppermute x32, starting transfers between devices, shifted(): lax.ppermute(value, axis, [(source, source + steps) for source in range(f...  108 us
    scatter-add x8, other arithmetic, add_points(): field_in.at[wave_index, place_at, row_index, col_index]  42.6 us
    add x18, other arithmetic, add_points(): field_in.at[wave_index, place_at, row_index, col_index]  11.6 us
    all_to_all x2, waiting for transfers between devices, copy_for_each(): lax.all_to_all(jnp.broadcast_to(value[None], (size, *value.shape)), axis,...  9.45 us
    ppermute x32, waiting for transfers between devices, shifted(): lax.ppermute(value, axis, [(source, source + steps) for source in range(f...  8.83 us
    all_to_all x2, starting transfers between devices, copy_for_each(): lax.all_to_all(jnp.broadcast_to(value[None], (size, *value.shape)), axis,...  7.7 us
  transfers between devices with their start and end apart: 34, of which 9 were waited for; matrix products, arithmetic and copies ran while one was open for 28% of the time, Pallas kernels for 0%

commit v1 on v0

v1 whole, which is shorter than its diff:
```python
import functools

import jax
import jax.numpy as jnp
from jax import lax
from jax.experimental import pallas as pl
from jax.experimental.pallas import tpu as pltpu
from jax.sharding import PartitionSpec as P

MESH = pl.DeviceIdType.MESH
time_step = 0.15
GUARD = 8
SXX, SYY, SZZ, SXY, SXZ, SYZ = range(6)


def window_kernel(
    dims,
    fields_in,
    earth_in,
    source_depth,
    source_column,
    wavelet,
    receiver_depth,
    receiver_column,
    traces,
    out,
    vel,
    vel_halo,
    sig,
    sig_halo,
    mat,
    mat_halo,
    source_at,
    inject,
    press,
    image,
    partial,
    landed,
    load_sem,
    first_send,
    first_recv,
    step_send,
    step_recv,
    sum_send,
    sum_recv,
):
    slabs, shots, depth, rows, cols, steps, receivers = dims
    here = lax.axis_index("gz")
    shot = lax.axis_index("shot")
    top, bottom = here > 0, here < slabs - 1
    last = depth - 1
    body = pl.ds(GUARD, rows)
    after = pl.ds(GUARD + 1, rows)
    before = pl.ds(GUARD - 1, rows)
    lane = lax.broadcasted_iota(jnp.int32, (rows, cols), 1)
    row = lax.broadcasted_iota(jnp.int32, (rows, cols), 0)
    at_first, at_last = lane == 0, lane == cols - 1
    partners = (shot + 1 - 2 * lax.rem(shot, 2), shots - 1 - shot)

    def b_y(f):
        return f - jnp.where(at_first, 0.0, pltpu.roll(f, 1, 1))

    def f_y(f):
        return jnp.where(at_last, 0.0, pltpu.roll(f, cols - 1, 1)) - f

    loads = [
        pltpu.make_async_copy(
            fields_in.at[:, 3:9], sig.at[:, :, :, body, :], load_sem.at[0]
        ),
        pltpu.make_async_copy(
            fields_in.at[:, 0:3], vel.at[:, :, :, body, :], load_sem.at[1]
        ),
        pltpu.make_async_copy(earth_in, mat, load_sem.at[2]),
    ]
    for copy in loads:
        copy.start()

    vel_halo[...] = jnp.zeros_like(vel_halo)
    sig_halo[...] = jnp.zeros_like(sig_halo)
    mat_halo[...] = jnp.zeros_like(mat_halo)

    barrier = pltpu.get_barrier_semaphore()

    @pl.when(top)
    def _():
        pl.semaphore_signal(barrier, inc=1, device_id={"gz": here - 1}, device_id_type=MESH)

    @pl.when(bottom)
    def _():
        pl.semaphore_signal(barrier, inc=1, device_id={"gz": here + 1}, device_id_type=MESH)

    for partner in partners:
        pl.semaphore_signal(barrier, inc=1, device_id={"shot": partner}, device_id_type=MESH)

    edge = pl.ds(0, GUARD)
    tail = pl.ds(GUARD + rows, GUARD)
    zeros = jnp.zeros((GUARD, cols), jnp.float32)
    for ref, count in ((vel, 3), (sig, 6)):
        for w in range(2):
            for c in range(count):
                for z in range(depth):
                    ref[w, c, z, edge, :] = zeros
                    ref[w, c, z, tail, :] = zeros

    have_top = jnp.where(top, 1, 0)
    have_bottom = jnp.where(bottom, 1, 0)
    pl.semaphore_wait(barrier, 2 + have_top + have_bottom)

    def remote(src, dst, send, recv, **to):
        return pltpu.make_async_remote_copy(
            src_ref=src, dst_ref=dst, send_sem=send, recv_sem=recv, device_id=to, device_id_type=MESH
        )

    first_down = [
        remote(fields_in.at[:, 7:9, last], sig_halo.at[:, 0:2], first_send.at[0], first_recv.at[0], gz=here + 1),
        remote(earth_in.at[2, last], mat_halo.at[0], first_send.at[1], first_recv.at[1], gz=here + 1),
    ]
    first_up = [
        remote(fields_in.at[:, 5, 0], sig_halo.at[:, 2], first_send.at[2], first_recv.at[2], gz=here - 1),
        remote(earth_in.at[1:3, 0], mat_halo.at[1:3], first_send.at[3], first_recv.at[3], gz=here - 1),
    ]

    @pl.when(bottom)
    def _():
        for copy in first_down:
            copy.start()

    @pl.when(top)
    def _():
        for copy in first_up:
            copy.start()

    def velocity_copies(w, slot):
        down = remote(
            vel.at[w, :, last, body, :],
            vel_halo.at[slot, 0, w, :, body, :],
            step_send.at[slot, 0, w],
            step_recv.at[slot, 0, w],
            gz=here + 1,
        )
        up = remote(
            vel.at[w, :, 0, body, :],
            vel_halo.at[slot, 1, w, :, body, :],
            step_send.at[slot, 1, w],
            step_recv.at[slot, 1, w],
            gz=here - 1,
        )
        return down, up

    def send_velocity(w, slot):
        down, up = velocity_copies(w, slot)

        @pl.when(bottom)
        def _():
            down.start()

        @pl.when(top)
        def _():
            up.start()

    def velocity_arrived(w, slot):
        down, up = velocity_copies(w, slot)

        @pl.when(top)
        def _():
            down.wait_recv()

        @pl.when(bottom)
        def _():
            up.wait_recv()

    def velocity_left(w, slot):
        down, up = velocity_copies(w, slot)

        @pl.when(bottom)
        def _():
            down.wait_send()

        @pl.when(top)
        def _():
            up.wait_send()

    source_row = (source_depth[0] - here * depth) * rows + source_column[0] // cols
    source_col = source_column[0] % cols
    for z in range(depth + 1):
        hit = (row + z * rows == source_row) & (lane == source_col)
        source_at[z] = jnp.where(hit, time_step, 0.0)
    cells = depth * rows
    receiver_row = (receiver_depth[...] - here * depth) * rows + receiver_column[...] // cols
    receiver_col = receiver_column[...] % cols
    in_row = lax.broadcasted_iota(jnp.int32, (cells, receivers), 0) == receiver_row
    in_col = lax.broadcasted_iota(jnp.int32, (cols, receivers), 0) == receiver_col
    in_col = jnp.where(in_col, 1.0, 0.0)
    for n in range(steps):
        amount = jnp.where(in_row, time_step * traces[0, pl.ds(n, 1), :], 0.0)
        inject[n] = lax.dot_general(
            amount,
            in_col,
            (((1,), (1,)), ((), ())),
            precision=lax.Precision.HIGHEST,
            preferred_element_type=jnp.float32,
        ).reshape(depth, rows, cols)
    image[...] = jnp.zeros_like(image)

    for copy in loads:
        copy.wait()
    mat[...] = time_step * mat[...]

    @pl.when(top)
    def _():
        for copy in first_down:
            copy.wait_recv()

    @pl.when(bottom)
    def _():
        for copy in first_up:
            copy.wait_recv()

    mat_halo[...] = time_step * mat_halo[...]

    def update_velocity(w, z, n):
        buoyancy = mat[0, z]
        sxx, syy, szz, sxy, sxz, syz = [sig[w, c, z, body, :] for c in range(6)]
        sxz_low = sig_halo[w, 0] if z == 0 else sig[w, SXZ, z - 1, body, :]
        syz_low = sig_halo[w, 1] if z == 0 else sig[w, SYZ, z - 1, body, :]
        szz_high = sig_halo[w, 2] if z == last else sig[w, SZZ, z + 1, body, :]
        fx = (sig[w, SXX, z, after, :] - sxx) + b_y(sxy) + (sxz - sxz_low)
        fy = (sxy - sig[w, SXY, z, before, :]) + f_y(syy) + (syz - syz_low)
        fz = (sxz - sig[w, SXZ, z, before, :]) + b_y(syz) + (szz_high - szz)
        vel[w, 0, z, body, :] = vel[w, 0, z, body, :] + buoyancy * fx
        vel[w, 1, z, body, :] = vel[w, 1, z, body, :] + buoyancy * fy
        moved = vel[w, 2, z, body, :] + buoyancy * fz
        if w == 1:
            moved = moved + inject[n, z]
        vel[w, 2, z, body, :] = moved

    def update_normal(w, z, n, slot):
        vx, vy, vz = [vel[w, c, z, body, :] for c in range(3)]
        vz_low = vel_halo[slot, 0, w, 2, body, :] if z == 0 else vel[w, 2, z - 1, body, :]
        ex = vx - vel[w, 0, z, before, :]
        ey = b_y(vy)
        ez = vz - vz_low
        common = mat[1, z] * (ex + ey + ez)
        twice = 2.0 * mat[2, z]
        if w == 0:
            common = common + source_at[z] * wavelet[0, n]
        sxx = sig[w, SXX, z, body, :] + (common + twice * ex)
        syy = sig[w, SYY, z, body, :] + (common + twice * ey)
        szz = sig[w, SZZ, z, body, :] + (common + twice * ez)
        sig[w, SXX, z, body, :] = sxx
        sig[w, SYY, z, body, :] = syy
        sig[w, SZZ, z, body, :] = szz
        pressure = (sxx + syy + szz) * (1.0 / 3.0)
        if w == 0:
            press[z] = pressure
        else:
            image[0, z] = image[0, z] + press[z] * pressure

    def update_shear(w, z, slot):
        vx, vy, vz = [vel[w, c, z, body, :] for c in range(3)]
        vx_high = vel_halo[slot, 1, w, 0, body, :] if z == last else vel[w, 0, z + 1, body, :]
        vy_high = vel_halo[slot, 1, w, 1, body, :] if z == last else vel[w, 1, z + 1, body, :]
        x_up = vx_high - vx
        y_up = vy_high - vy
        z_along_x = vel[w, 2, z, after, :] - vz
        z_along_y = f_y(vz)
        x_along_y = f_y(vx)
        y_along_x = vel[w, 1, z, after, :] - vy
        mu = mat[2, z]
        sig[w, SXY, z, body, :] = sig[w, SXY, z, body, :] + mu * (x_along_y + y_along_x)
        sig[w, SXZ, z, body, :] = sig[w, SXZ, z, body, :] + mu * (x_up + z_along_x)
        sig[w, SYZ, z, body, :] = sig[w, SYZ, z, body, :] + mu * (y_up + z_along_y)
        if w == 1:
            rotation = (z_along_y - y_up) + (x_up - z_along_x) + (y_along_x - x_along_y)
            image[1, z] = image[1, z] + press[z] * rotation

    def update_halo(w, n, slot):
        vx, vy, vz = [vel_halo[slot, 0, w, c, body, :] for c in range(3)]
        mu = mat_halo[0]
        x_term = (vel[w, 0, 0, body, :] - vx) + (vel_halo[slot, 0, w, 2, after, :] - vz)
        y_term = (vel[w, 1, 0, body, :] - vy) + f_y(vz)
        sig_halo[w, 0] = sig_halo[w, 0] + mu * x_term
        sig_halo[w, 1] = sig_halo[w, 1] + mu * y_term
        vx, vy, vz = [vel_halo[slot, 1, w, c, body, :] for c in range(3)]
        ex = vx - vel_halo[slot, 1, w, 0, before, :]
        ez = vz - vel[w, 2, last, body, :]
        change = mat_halo[1] * (ex + b_y(vy) + ez) + 2.0 * mat_halo[2] * ez
        if w == 0:
            change = change + source_at[depth] * wavelet[0, n]
        sig_halo[w, 2] = sig_halo[w, 2] + change

    inner = range(1, last)

    def stress_inside(n, slot):
        for w in range(2):
            for z in range(1, depth):
                update_normal(w, z, n, slot)
            if w == 0:
                for z in range(last):
                    update_shear(w, z, slot)
            else:
                for z in range(1, last):
                    update_shear(w, z, slot)

    def stress_edge(w, n, slot):
        update_normal(w, 0, n, slot)
        if w == 1:
            update_shear(w, 0, slot)
        update_shear(w, last, slot)

    for w in range(2):
        update_velocity(w, 0, 0)
        update_velocity(w, last, 0)
        send_velocity(w, 0)
    for w in range(2):
        for z in inner:
            update_velocity(w, z, 0)

    def step(n, carry):
        slot = lax.rem(n, 2)
        stress_inside(n, slot)
        for w in range(2):
            velocity_arrived(w, slot)
            stress_edge(w, n, slot)
            update_halo(w, n, slot)
            velocity_left(w, slot)
            update_velocity(w, 0, n + 1)
            update_velocity(w, last, n + 1)
            send_velocity(w, 1 - slot)
        for w in range(2):
            for z in inner:
                update_velocity(w, z, n + 1)
        return carry

    lax.fori_loop(0, steps - 1, step, 0)

    end = steps - 1
    slot = end % 2
    stress_inside(end, slot)
    for w in range(2):
        velocity_arrived(w, slot)
        stress_edge(w, end, slot)
        velocity_left(w, slot)

    first_round = [
        remote(image.at[i], landed.at[0, i], sum_send.at[0, i], sum_recv.at[0, i], shot=partners[i])
        for i in range(2)
    ]
    second_round = [
        remote(partial.at[i], landed.at[1, i], sum_send.at[1, i], sum_recv.at[1, i], shot=partners[1 - i])
        for i in range(2)
    ]
    for i in range(2):
        first_round[i].start()
    for i in range(2):
        first_round[i].wait_recv()
        partial[i] = image[i] + landed[0, i]
        second_round[i].start()
    for i in range(2):
        second_round[i].wait_recv()
        out[i] = partial[i] + landed[1, i]
    for i in range(2):
        first_round[i].wait_send()
        second_round[i].wait_send()

    @pl.when(bottom)
    def _():
        for copy in first_down:
            copy.wait_send()

    @pl.when(top)
    def _():
        for copy in first_up:
            copy.wait_send()


def solution(mesh):
    slabs, shots = mesh.shape["gz"], mesh.shape["shot"]

    def on_device(wavefields, earth, s_depth, s_column, wavelet, r_depth, r_column, traces):
        depth, rows, cols = earth.shape[1:]
        steps, receivers = traces.shape[1:]
        dims = (slabs, shots, depth, rows, cols, steps, receivers)
        padded = rows + 2 * GUARD
        f32 = jnp.float32
        any_spec = pl.BlockSpec(memory_space=pl.ANY)
        smem = pl.BlockSpec(memory_space=pltpu.SMEM)
        vmem = pl.BlockSpec(memory_space=pltpu.VMEM)
        dma = pltpu.SemaphoreType.DMA
        summed = pl.pallas_call(
            functools.partial(window_kernel, dims),
            out_shape=jax.ShapeDtypeStruct((2, depth, rows, cols), f32),
            in_specs=[any_spec, any_spec, smem, smem, smem, vmem, vmem, vmem],
            out_specs=vmem,
            scratch_shapes=[
                pltpu.VMEM((2, 3, depth, padded, cols), f32),
                pltpu.VMEM((2, 2, 2, 3, padded, cols), f32),
                pltpu.VMEM((2, 6, depth, padded, cols), f32),
                pltpu.VMEM((2, 3, rows, cols), f32),
                pltpu.VMEM((3, depth, rows, cols), f32),
                pltpu.VMEM((3, rows, cols), f32),
                pltpu.VMEM((depth + 1, rows, cols), f32),
                pltpu.VMEM((steps, depth, rows, cols), f32),
                pltpu.VMEM((depth, rows, cols), f32),
                pltpu.VMEM((2, depth, rows, cols), f32),
                pltpu.VMEM((2, depth, rows, cols), f32),
                pltpu.VMEM((2, 2, depth, rows, cols), f32),
                dma((3,)),
                dma((4,)),
                dma((4,)),
                dma((2, 2, 2)),
                dma((2, 2, 2)),
                dma((2, 2)),
                dma((2, 2)),
            ],
            compiler_params=pltpu.CompilerParams(collective_id=0, has_side_effects=True),
        )(wavefields[0], earth, s_depth, s_column, wavelet, r_depth, r_column, traces)
        return summed / steps

    sharded = P(("parts", "shot"))
    return jax.shard_map(
        on_device,
        mesh=mesh,
        in_specs=(
            P(("parts", "shot"), None, None, "gz", None, None),
            P("parts", "gz", None, None),
            sharded,
            sharded,
            P(("parts", "shot"), None),
            P(("parts", "shot"), None),
            P(("parts", "shot"), None),
            P(("parts", "shot"), None, None),
        ),
        out_specs=P("parts", "gz", None, None),
        check_vma=False,
    )
```

time: 282 us -> 57.2 us (0.20); the launches traced: 278 us -> 57 us
  starting transfers between devices: 115 us -> 0 us
  other arithmetic: 74.2 us -> 1.57 us
  Pallas kernels: 0 us -> 54.1 us
  between operations: 53 us -> 1.3 us
  waiting for transfers between devices: 18.3 us -> 0 us
  local copies, waits for them, and re-layouts: 17.2 us -> 0 us
    ppermute x32 -> x0, starting transfers between devices: 108 us -> none  [shifted(): lax.ppermute(value, axis, [(source, source + steps) for source in range(f...]
    pallas_call x0 -> x1, Pallas kernels: none -> 54.1 us  [on_device(): pl.pallas_call(functools.partial(window_kernel, dims), out_shape=jax.Shap...]
    scatter-add x8 -> x0, other arithmetic: 42.6 us -> none  [add_points(): field_in.at[wave_index, place_at, row_index, col_index]]
    add x60 -> x0, other arithmetic: 24.8 us -> none  [the longest x18 11.6 us: add_points(): field_in.at[wave_index, place_at, row_index, col_index]]
    all_to_all x2 -> x0, waiting for transfers between devices: 9.45 us -> none  [copy_for_each(): lax.all_to_all(jnp.broadcast_to(value[None], (size, *value.shape)), axis,...]
    ppermute x32 -> x0, waiting for transfers between devices: 8.83 us -> none  [shifted(): lax.ppermute(value, axis, [(source, source + steps) for source in range(f...]
    all_to_all x2 -> x0, starting transfers between devices: 7.7 us -> none  [copy_for_each(): lax.all_to_all(jnp.broadcast_to(value[None], (size, *value.shape)), axis,...]
    another operation x53 -> x0, local copies, waits for them, and re-layouts: 4.7 us -> none
  transfers between devices with their start and end apart: 34 -> 0, of which waited for: 9 -> 0; matrix products, arithmetic and copies ran while one was open for 28% -> 0% of each run, Pallas kernels for 0% -> 0%
where the time goes in v1:
time: 57.2 us; the launch traced here: 57 us
  Pallas kernels  54.1 us (95%)
  other arithmetic  1.57 us (3%)
  between operations  1.3 us (2%)
    pallas_call x1, Pallas kernels, on_device(): pl.pallas_call(functools.partial(window_kernel, dims), out_shape=jax.Shap...  54.1 us
    div x1, other arithmetic, on_device(): return summed / steps  1.57 us

profile of v1, /device:TPU:33, one launch (start us, length us, event | category | flops | bytes accessed | tf_op | source)
XLA Modules:
  0.0 57.0 jit_solution(5271256979532804162)
XLA Ops:
  1.3 54.1 %shard_map.82 = f32[2,4,32,128]{3,2,1,0:T(8,128)} custom-call(f32[2,9,4,32,128]{4,3,2,1,0:T(8,128)} %bitcast.1, f32[3,4,32,128]{3,2,1,0:T(8,128)} %earth_in.1, s32[1]{0:T(128)S(6)} %copy.9.source_depth, s32[1]{0:T(128)S(6)} %copy.10.source_column, f32[1,8]{1,0:T(1,128)} %wavelet.1, s32[1,64]{1,0:T(1,128)} %receiver_depth.1, s32[1,64]{1,0:T(1,128)} %receiver_column.1, ...), custom_call_target="tpu_custom_call" | custom-call | tf_op jit(solution)/shard_map/pallas_call | solution.py:390
  55.4 1.6 %broadcast_multiply_fusion = f32[2,4,32,128]{3,2,1,0:T(8,128)} fusion(f32[2,4,32,128]{3,2,1,0:T(8,128)} %shard_map.82), kind=kLoop, calls=%fused_computation | loop fusion | flops 32768 | bytes 262144 | tf_op jit(solution)/shard_map/div | solution.py:418

commit v2 on v1

v2 whole, which is shorter than its diff:
```python
import functools

import jax
import jax.numpy as jnp
from jax import lax
from jax.experimental import pallas as pl
from jax.experimental.pallas import tpu as pltpu
from jax.sharding import PartitionSpec as P

MESH = pl.DeviceIdType.MESH
time_step = 0.15
GUARD = 8
SXX, SYY, SZZ, SXY, SXZ, SYZ = range(6)


def window_kernel(
    dims,
    fields_in,
    earth_in,
    source_depth_in,
    source_column_in,
    wavelet_in,
    receiver_depth_in,
    receiver_column_in,
    traces_in,
    out,
    vel,
    vel_msg,
    vel_mid,
    vel_near,
    sig,
    sig_near,
    sig_far,
    mat,
    mat_near,
    mat_far,
    source_at,
    inject,
    press,
    spin,
    image,
    partial,
    landed,
    source_depth,
    source_column,
    wavelet,
    receiver_depth,
    receiver_column,
    traces,
    load_sem,
    small_sem,
    first_send,
    first_recv,
    msg_send,
    msg_recv,
    mid_send,
    mid_recv,
    sum_send,
    sum_recv,
):
    slabs, shots, depth, rows, cols, steps, receivers = dims
    here = lax.axis_index("gz")
    shot = lax.axis_index("shot")
    has_up, has_down = here > 0, here < slabs - 1
    last = depth - 1
    whole = pl.ds(0, rows)
    body = pl.ds(GUARD, rows)
    after = pl.ds(GUARD + 1, rows)
    before = pl.ds(GUARD - 1, rows)
    lane = lax.broadcasted_iota(jnp.int32, (rows, cols), 1)
    row = lax.broadcasted_iota(jnp.int32, (rows, cols), 0)
    at_first, at_last = lane == 0, lane == cols - 1
    partners = (shot + 1 - 2 * lax.rem(shot, 2), shots - 1 - shot)

    def b_y(f):
        return f - jnp.where(at_first, 0.0, pltpu.roll(f, 1, 1))

    def f_y(f):
        return jnp.where(at_last, 0.0, pltpu.roll(f, cols - 1, 1)) - f

    loads = [
        pltpu.make_async_copy(
            fields_in.at[:, 3:9], sig.at[:, :, :, body, :], load_sem.at[0]
        ),
        pltpu.make_async_copy(
            fields_in.at[:, 0:3], vel.at[1, :, :, :, body, :], load_sem.at[1]
        ),
        pltpu.make_async_copy(earth_in, mat, load_sem.at[2]),
    ]
    small = [
        pltpu.make_async_copy(src, dst, small_sem.at[i])
        for i, (src, dst) in enumerate(
            (
                (source_depth_in, source_depth),
                (source_column_in, source_column),
                (wavelet_in, wavelet),
                (receiver_depth_in, receiver_depth),
                (receiver_column_in, receiver_column),
                (traces_in, traces),
            )
        )
    ]
    for copy in loads + small:
        copy.start()

    for ref in (vel_msg, vel_mid, sig_near, sig_far, mat_near, mat_far):
        ref[...] = jnp.zeros_like(ref)

    barrier = pltpu.get_barrier_semaphore()

    def up_to(where, then):
        @pl.when(where)
        def _():
            then()

    def greet(**to):
        pl.semaphore_signal(barrier, inc=1, device_id=to, device_id_type=MESH)

    up_to(has_down, lambda: greet(gz=here + 1))
    up_to(has_up, lambda: greet(gz=here - 1))
    for partner in partners:
        greet(shot=partner)

    edge = pl.ds(0, GUARD)
    tail = pl.ds(GUARD + rows, GUARD)
    zeros = jnp.zeros((GUARD, cols), jnp.float32)
    for w in range(2):
        for z in range(depth):
            for c in range(6):
                sig[w, c, z, edge, :] = zeros
                sig[w, c, z, tail, :] = zeros
            for c in range(3):
                for parity in range(2):
                    vel[parity, w, c, z, edge, :] = zeros
                    vel[parity, w, c, z, tail, :] = zeros
        for c in range(3):
            for side in range(2):
                vel_near[side, w, c, edge, :] = zeros
                vel_near[side, w, c, tail, :] = zeros

    pl.semaphore_wait(barrier, 2 + jnp.where(has_up, 1, 0) + jnp.where(has_down, 1, 0))

    def remote(src, dst, send, recv, **to):
        return pltpu.make_async_remote_copy(
            src_ref=src, dst_ref=dst, send_sem=send, recv_sem=recv, device_id=to, device_id_type=MESH
        )

    downs = (
        (fields_in.at[:, 7:9, last], sig_near.at[0, :, 4:6, body, :]),
        (fields_in.at[:, 3:7, last], sig_near.at[0, :, 0:4, body, :]),
        (fields_in.at[:, 7:9, last - 1], sig_far.at[:, 0:2]),
        (earth_in.at[:, last], mat_near.at[0]),
        (earth_in.at[2, last - 1], mat_far.at[0]),
    )
    ups = (
        (fields_in.at[:, 5:6, 0], sig_near.at[1, :, 2:3, body, :]),
        (fields_in.at[:, 3:5, 0], sig_near.at[1, :, 0:2, body, :]),
        (fields_in.at[:, 6:9, 0], sig_near.at[1, :, 3:6, body, :]),
        (fields_in.at[:, 5, 1], sig_far.at[:, 2]),
        (earth_in.at[:, 0], mat_near.at[1]),
        (earth_in.at[1:3, 1], mat_far.at[1:3]),
    )
    first_down = [
        remote(src, dst, first_send.at[0, i], first_recv.at[0, i], gz=here + 1)
        for i, (src, dst) in enumerate(downs)
    ]
    first_up = [
        remote(src, dst, first_send.at[1, i], first_recv.at[1, i], gz=here - 1)
        for i, (src, dst) in enumerate(ups)
    ]
    up_to(has_down, lambda: [copy.start() for copy in first_down])
    up_to(has_up, lambda: [copy.start() for copy in first_up])

    def message(w, slot, side):
        planes = pl.ds(depth - 2, 2) if side == 0 else pl.ds(0, 2)
        return remote(
            vel.at[0, w, :, planes, body, :],
            vel_msg.at[slot, side, w, :, :, body, :],
            msg_send.at[slot, side, w],
            msg_recv.at[slot, side, w],
            gz=here + 1 if side == 0 else here - 1,
        )

    def middle(w, cycle, side):
        return remote(
            vel.at[1, w, :, depth - 2 if side == 0 else 1, body, :],
            vel_mid.at[cycle, side, w, :, body, :],
            mid_send.at[cycle, side, w],
            mid_recv.at[cycle, side, w],
            gz=here + 1 if side == 0 else here - 1,
        )

    goes = (has_down, has_up)
    comes = (has_up, has_down)

    for copy in small:
        copy.wait()
    source_row = (source_depth[0] - here * depth + 1) * rows + source_column[0] // cols
    source_col = source_column[0] % cols
    for z in range(depth + 3):
        hit = (row + z * rows == source_row) & (lane == source_col)
        source_at[z] = jnp.where(hit, time_step, 0.0)
    cells = (depth + 2) * rows
    receiver_row = (receiver_depth[...] - here * depth + 1) * rows + receiver_column[...] // cols
    receiver_col = receiver_column[...] % cols
    in_row = lax.broadcasted_iota(jnp.int32, (cells, receivers), 0) == receiver_row
    in_col = lax.broadcasted_iota(jnp.int32, (cols, receivers), 0) == receiver_col
    in_col = jnp.where(in_col, 1.0, 0.0)

    def receivers_at(n, carry):
        amount = jnp.where(in_row, time_step * traces[0, pl.ds(n, 1), :], 0.0)
        inject[n] = lax.dot_general(
            amount,
            in_col,
            (((1,), (1,)), ((), ())),
            precision=lax.Precision.HIGHEST,
            preferred_element_type=jnp.float32,
        ).reshape(depth + 2, rows, cols)
        return carry

    lax.fori_loop(0, steps, receivers_at, 0)
    image[...] = jnp.zeros_like(image)

    for copy in loads:
        copy.wait()
    mat[...] = time_step * mat[...]

    def v(parity, slot, w, c, e, at=body):
        if 0 <= e < depth:
            return vel[parity, w, c, e, at, :]
        side = 0 if e < 0 else 1
        if parity == 0:
            return vel_msg[slot, side, w, c, e + 2 if e < 0 else e - depth, at, :]
        if e in (-1, depth):
            return vel_near[side, w, c, at, :]
        return vel_mid[slot, side, w, c, at, :]

    def s_at(w, f, e):
        if 0 <= e < depth:
            return sig, (w, f, e), True
        if e in (-1, depth):
            return sig_near, (0 if e < 0 else 1, w, f), True
        return sig_far, (w, {SXZ: 0, SYZ: 1, SZZ: 2}[f]), False

    def s(w, f, e, at=body):
        ref, index, guarded = s_at(w, f, e)
        return ref[(*index, at if guarded else whole, slice(None))]

    def add_s(w, f, e, change):
        ref, index, guarded = s_at(w, f, e)
        value = ref[(*index, body if guarded else whole, slice(None))] + change
        ref[(*index, body if guarded else whole, slice(None))] = value
        return value

    def m(which, e):
        if 0 <= e < depth:
            return mat[which, e]
        if e in (-1, depth):
            return mat_near[0 if e < 0 else 1, which]
        return mat_far[0 if e < 0 else which]

    def velocity(w, e, n, old, slot):
        sxx, syy, szz, sxy, sxz, syz = [s(w, f, e) for f in range(6)]
        fx = (s(w, SXX, e, after) - sxx) + b_y(sxy) + (sxz - s(w, SXZ, e - 1))
        fy = (sxy - s(w, SXY, e, before)) + f_y(syy) + (syz - s(w, SYZ, e - 1))
        fz = (sxz - s(w, SXZ, e, before)) + b_y(syz) + (s(w, SZZ, e + 1) - szz)
        buoyancy = m(0, e)
        moved = [v(old, slot, w, c, e) + buoyancy * f for c, f in enumerate((fx, fy, fz))]
        if w == 1:
            moved[2] = moved[2] + inject[n, e + 1]
        for c in range(3):
            if 0 <= e < depth:
                vel[1 - old, w, c, e, body, :] = moved[c]
            else:
                vel_near[0 if e < 0 else 1, w, c, body, :] = moved[c]

    def normal(parity, slot, w, e, n, spun=None):
        vx, vy, vz = [v(parity, slot, w, c, e) for c in range(3)]
        ex = vx - v(parity, slot, w, 0, e, before)
        ey = b_y(vy)
        ez = vz - v(parity, slot, w, 2, e - 1)
        common = m(1, e) * (ex + ey + ez)
        twice = 2.0 * m(2, e)
        if w == 0:
            common = common + source_at[e + 1] * wavelet[0, n]
        szz = add_s(w, SZZ, e, common + twice * ez)
        if e > depth:
            return
        sxx = add_s(w, SXX, e, common + twice * ex)
        syy = add_s(w, SYY, e, common + twice * ey)
        if not 0 <= e < depth:
            return
        pressure = (sxx + syy + szz) * (1.0 / 3.0)
        if w == 0:
            press[parity, e] = pressure
        else:
            image[0, e] = image[0, e] + press[parity, e] * pressure
            if spun is not None:
                image[1, e] = image[1, e] + press[parity, e] * spin[spun]

    def shear(parity, slot, w, e, spun=None):
        vx, vy, vz = [v(parity, slot, w, c, e) for c in range(3)]
        x_up = v(parity, slot, w, 0, e + 1) - vx
        y_up = v(parity, slot, w, 1, e + 1) - vy
        z_along_x = v(parity, slot, w, 2, e, after) - vz
        z_along_y = f_y(vz)
        x_along_y = f_y(vx)
        y_along_x = v(parity, slot, w, 1, e, after) - vy
        mu = m(2, e)
        add_s(w, SXY, e, mu * (x_along_y + y_along_x))
        add_s(w, SXZ, e, mu * (x_up + z_along_x))
        add_s(w, SYZ, e, mu * (y_up + z_along_y))
        if w == 1:
            rotation = (z_along_y - y_up) + (x_up - z_along_x) + (y_along_x - x_along_y)
            if spun is None:
                image[1, e] = image[1, e] + press[parity, e] * rotation
            else:
                spin[spun] = rotation

    def shear_flat(parity, slot, w, e):
        x_along_y = f_y(v(parity, slot, w, 0, e))
        y_along_x = v(parity, slot, w, 1, e, after) - v(parity, slot, w, 1, e)
        add_s(w, SXY, e, m(2, e) * (x_along_y + y_along_x))

    def shear_deep(parity, slot, w, e):
        vx, vy, vz = [v(parity, slot, w, c, e) for c in range(3)]
        mu = m(2, e)
        z_along_x = v(parity, slot, w, 2, e, after) - vz
        add_s(w, SXZ, e, mu * ((v(parity, slot, w, 0, e + 1) - vx) + z_along_x))
        add_s(w, SYZ, e, mu * ((v(parity, slot, w, 1, e + 1) - vy) + f_y(vz)))

    def inside(cycle, n, send):
        for w in range(2):
            for e in range(1, depth):
                normal(0, None, w, e, n)
            shear(0, None, w, 0, spun=0)
            for e in range(1, last):
                shear(0, None, w, e)
            for e in (1, 2):
                velocity(w, e, n + 1, 0, None)

            def start(w=w):
                for side in range(2):
                    up_to(goes[side], middle(w, cycle, side).start)

            if send is True:
                start()
            else:
                up_to(send, start)
            normal(1, None, w, 2, n + 1)
            shear(1, None, w, 1, spun=1)

    def lower(slot, w, n, final):
        up_to(comes[1], message(w, slot, 1).wait_recv)
        shear(0, slot, w, last)
        normal(0, slot, w, depth, n)
        shear_flat(0, slot, w, depth)
        shear_deep(0, slot, w, depth)
        normal(0, slot, w, depth + 1, n)
        velocity(w, last, n + 1, 0, slot)
        velocity(w, depth, n + 1, 0, slot)
        normal(1, slot, w, last, n + 1)
        shear(1, slot, w, last - 1)
        shear(1, slot, w, last)
        up_to(goes[0], message(w, slot, 0).wait_send)
        if final:
            return
        normal(1, slot, w, depth, n + 1)
        velocity(w, last, n + 2, 1, slot)
        velocity(w, last - 1, n + 2, 1, slot)
        up_to(goes[0], message(w, 1 - slot, 0).start)
        shear_flat(1, slot, w, depth)

    def upper(slot, w, n, final):
        up_to(comes[0], message(w, slot, 0).wait_recv)
        normal(0, slot, w, 0, n, spun=0)
        shear_deep(0, slot, w, -1)
        shear_flat(0, slot, w, -1)
        normal(0, slot, w, -1, n)
        shear_deep(0, slot, w, -2)
        velocity(w, 0, n + 1, 0, slot)
        velocity(w, -1, n + 1, 0, slot)
        normal(1, slot, w, 0, n + 1)
        normal(1, slot, w, 1, n + 1, spun=1)
        shear(1, slot, w, 0)
        up_to(goes[1], message(w, slot, 1).wait_send)
        if final:
            return
        shear_deep(1, slot, w, -1)
        velocity(w, 0, n + 2, 1, slot)
        velocity(w, 1, n + 2, 1, slot)
        up_to(goes[1], message(w, 1 - slot, 1).start)
        shear_flat(1, slot, w, -1)

    def catch_up(cycle, n):
        for w in range(2):
            up_to(comes[1], middle(w, cycle, 1).wait_recv)
            shear_deep(1, cycle, w, depth)
            normal(1, cycle, w, depth + 1, n)
            up_to(comes[0], middle(w, cycle, 0).wait_recv)
            normal(1, cycle, w, -1, n)
            shear_deep(1, cycle, w, -2)

    up_to(comes[1], first_up[0].wait_recv)
    for w in range(2):
        velocity(w, last, 0, 1, None)
        velocity(w, last - 1, 0, 1, None)
        up_to(goes[0], message(w, 0, 0).start)
    up_to(comes[0], first_down[0].wait_recv)
    for w in range(2):
        velocity(w, 0, 0, 1, None)
        velocity(w, 1, 0, 1, None)
        up_to(goes[1], message(w, 0, 1).start)
    inside(0, 0, True)
    up_to(comes[1], lambda: [copy.wait_recv() for copy in first_up[1:]])
    up_to(comes[0], lambda: [copy.wait_recv() for copy in first_down[1:]])
    mat_near[...] = time_step * mat_near[...]
    mat_far[...] = time_step * mat_far[...]

    cycles = steps // 2

    def cycle_body(cycle, carry):
        slot = lax.rem(cycle, 2)
        n = 2 * cycle
        for w in range(2):
            lower(slot, w, n, False)
        for w in range(2):
            upper(slot, w, n, False)
        for w in range(2):
            for side in range(2):
                up_to(goes[side], middle(w, cycle, side).wait_send)
        inside(cycle + 1, n + 2, cycle < cycles - 2)
        catch_up(cycle, n + 1)
        return carry

    lax.fori_loop(0, cycles - 1, cycle_body, 0)

    def first_round(half, i):
        planes = pl.ds(2 * half, 2)
        return remote(
            image.at[i, planes],
            landed.at[0, i, planes],
            sum_send.at[0, half, i],
            sum_recv.at[0, half, i],
            shot=partners[i],
        )

    def second_round(half, i):
        planes = pl.ds(2 * half, 2)
        return remote(
            partial.at[i, planes],
            landed.at[1, i, planes],
            sum_send.at[1, half, i],
            sum_recv.at[1, half, i],
            shot=partners[1 - i],
        )

    end = (cycles - 1) % 2
    for w in range(2):
        lower(end, w, steps - 2, True)
    for i in range(2):
        first_round(1, i).start()
    for w in range(2):
        upper(end, w, steps - 2, True)
    for i in range(2):
        first_round(0, i).start()
    for half in (1, 0):
        planes = pl.ds(2 * half, 2)
        for i in range(2):
            first_round(half, i).wait_recv()
            partial[i, planes] = image[i, planes] + landed[0, i, planes]
            second_round(half, i).start()
    for half in (1, 0):
        planes = pl.ds(2 * half, 2)
        for i in range(2):
            second_round(half, i).wait_recv()
            out[i, planes] = partial[i, planes] + landed[1, i, planes]
    for half in (1, 0):
        for i in range(2):
            first_round(half, i).wait_send()
            second_round(half, i).wait_send()
    up_to(has_down, lambda: [copy.wait_send() for copy in first_down])
    up_to(has_up, lambda: [copy.wait_send() for copy in first_up])


def solution(mesh):
    slabs, shots = mesh.shape["gz"], mesh.shape["shot"]

    def on_device(wavefields, earth, s_depth, s_column, wavelet, r_depth, r_column, traces):
        depth, rows, cols = earth.shape[1:]
        steps, receivers = traces.shape[1:]
        assert depth == 4 and shots == 4 and steps % 2 == 0 and steps >= 4
        dims = (slabs, shots, depth, rows, cols, steps, receivers)
        padded = rows + 2 * GUARD
        f32 = jnp.float32
        mids = steps // 2 - 1
        hbm = pl.BlockSpec(memory_space=pltpu.HBM)
        vmem = pl.BlockSpec(memory_space=pltpu.VMEM)
        dma = pltpu.SemaphoreType.DMA
        summed = pl.pallas_call(
            functools.partial(window_kernel, dims),
            out_shape=jax.ShapeDtypeStruct((2, depth, rows, cols), f32),
            in_specs=[hbm] * 8,
            out_specs=vmem,
            scratch_shapes=[
                pltpu.VMEM((2, 2, 3, depth, padded, cols), f32),
                pltpu.VMEM((2, 2, 2, 3, 2, padded, cols), f32),
                pltpu.VMEM((mids, 2, 2, 3, padded, cols), f32),
                pltpu.VMEM((2, 2, 3, padded, cols), f32),
                pltpu.VMEM((2, 6, depth, padded, cols), f32),
                pltpu.VMEM((2, 2, 6, padded, cols), f32),
                pltpu.VMEM((2, 3, rows, cols), f32),
                pltpu.VMEM((3, depth, rows, cols), f32),
                pltpu.VMEM((2, 3, rows, cols), f32),
                pltpu.VMEM((3, rows, cols), f32),
                pltpu.VMEM((depth + 3, rows, cols), f32),
                pltpu.VMEM((steps, depth + 2, rows, cols), f32),
                pltpu.VMEM((2, depth, rows, cols), f32),
                pltpu.VMEM((2, rows, cols), f32),
                pltpu.VMEM((2, depth, rows, cols), f32),
                pltpu.VMEM((2, depth, rows, cols), f32),
                pltpu.VMEM((2, 2, depth, rows, cols), f32),
                pltpu.SMEM(s_depth.shape, jnp.int32),
                pltpu.SMEM(s_column.shape, jnp.int32),
                pltpu.SMEM(wavelet.shape, f32),
                pltpu.VMEM(r_depth.shape, jnp.int32),
                pltpu.VMEM(r_column.shape, jnp.int32),
                pltpu.VMEM(traces.shape, f32),
                dma((3,)),
                dma((6,)),
                dma((2, 6)),
                dma((2, 6)),
                dma((2, 2, 2)),
                dma((2, 2, 2)),
                dma((mids, 2, 2)),
                dma((mids, 2, 2)),
                dma((2, 2, 2)),
                dma((2, 2, 2)),
            ],
            compiler_params=pltpu.CompilerParams(collective_id=0, has_side_effects=True),
        )(wavefields[0], earth, s_depth, s_column, wavelet, r_depth, r_column, traces)
        return summed / steps

    sharded = P(("parts", "shot"))
    return jax.shard_map(
        on_device,
        mesh=mesh,
        in_specs=(
            P(("parts", "shot"), None, None, "gz", None, None),
            P("parts", "gz", None, None),
            sharded,
            sharded,
            P(("parts", "shot"), None),
            P(("parts", "shot"), None),
            P(("parts", "shot"), None),
            P(("parts", "shot"), None, None),
        ),
        out_specs=P("parts", "gz", None, None),
        check_vma=False,
    )
```

time: 57.2 us -> 50.2 us (0.88)
  Pallas kernels: 54.1 us -> 47.1 us
    pallas_call x1, Pallas kernels: 54.1 us -> 47.1 us  [on_device(): pl.pallas_call(functools.partial(window_kernel, dims), out_shape=jax.Shap...]
where the time goes in v2:
time: 50.2 us; the launch traced here: 50 us
  Pallas kernels  47.1 us (94%)
  other arithmetic  1.57 us (3%)
  between operations  1.3 us (3%)
    pallas_call x1, Pallas kernels, on_device(): pl.pallas_call(functools.partial(window_kernel, dims), out_shape=jax.Shap...  47.1 us
    div x1, other arithmetic, on_device(): return summed / steps  1.57 us

profile of v2, /device:TPU:33, one launch (start us, length us, event | category | flops | bytes accessed | tf_op | source)
XLA Modules:
  0.0 50.0 jit_solution(9016454158388523599)
XLA Ops:
  1.3 47.1 %shard_map.82 = f32[2,4,32,128]{3,2,1,0:T(8,128)} custom-call(f32[2,9,4,32,128]{4,3,2,1,0:T(8,128)} %bitcast.1, f32[3,4,32,128]{3,2,1,0:T(8,128)} %earth_in.1, s32[1]{0:T(128)S(6)} %copy.9.source_depth_in, s32[1]{0:T(128)S(6)} %copy.10.source_column_in, f32[1,8]{1,0:T(1,128)} %wavelet_in.1, s32[1,64]{1,0:T(1,128)} %receiver_depth_in.1, ...), custom_call_target="tpu_custom_call" | custom-call | tf_op jit(solution)/shard_map/pallas_call | solution.py:500
  48.5 1.6 %broadcast_multiply_fusion = f32[2,4,32,128]{3,2,1,0:T(8,128)} fusion(f32[2,4,32,128]{3,2,1,0:T(8,128)} %shard_map.82), kind=kLoop, calls=%fused_computation | loop fusion | flops 32768 | bytes 262144 | tf_op jit(solution)/shard_map/div | solution.py:542

commit v3 on v2

--- a/solution.py
+++ b/solution.py
@@ -1,4 +1,5 @@
 import functools
+import itertools
 
 import jax
 import jax.numpy as jnp
@@ -39,8 +40,7 @@
     press,
     spin,
     image,
-    partial,
-    landed,
+    parts,
     source_depth,
     source_column,
     wavelet,
@@ -49,6 +49,7 @@
     traces,
     load_sem,
     small_sem,
+    keep_sem,
     first_send,
     first_recv,
     msg_send,
@@ -70,7 +71,6 @@
     lane = lax.broadcasted_iota(jnp.int32, (rows, cols), 1)
     row = lax.broadcasted_iota(jnp.int32, (rows, cols), 0)
     at_first, at_last = lane == 0, lane == cols - 1
-    partners = (shot + 1 - 2 * lax.rem(shot, 2), shots - 1 - shot)
 
     def b_y(f):
         return f - jnp.where(at_first, 0.0, pltpu.roll(f, 1, 1))
@@ -103,9 +103,6 @@
     for copy in loads + small:
         copy.start()
 
-    for ref in (vel_msg, vel_mid, sig_near, sig_far, mat_near, mat_far):
-        ref[...] = jnp.zeros_like(ref)
-
     barrier = pltpu.get_barrier_semaphore()
 
     def up_to(where, then):
@@ -118,27 +115,10 @@
 
     up_to(has_down, lambda: greet(gz=here + 1))
     up_to(has_up, lambda: greet(gz=here - 1))
-    for partner in partners:
-        greet(shot=partner)
-
-    edge = pl.ds(0, GUARD)
-    tail = pl.ds(GUARD + rows, GUARD)
-    zeros = jnp.zeros((GUARD, cols), jnp.float32)
-    for w in range(2):
-        for z in range(depth):
-            for c in range(6):
-                sig[w, c, z, edge, :] = zeros
-                sig[w, c, z, tail, :] = zeros
-            for c in range(3):
-                for parity in range(2):
-                    vel[parity, w, c, z, edge, :] = zeros
-                    vel[parity, w, c, z, tail, :] = zeros
-        for c in range(3):
-            for side in range(2):
-                vel_near[side, w, c, edge, :] = zeros
-                vel_near[side, w, c, tail, :] = zeros
-
-    pl.semaphore_wait(barrier, 2 + jnp.where(has_up, 1, 0) + jnp.where(has_down, 1, 0))
+    others = range(1, shots)
+    for hop in others:
+        greet(shot=lax.rem(shot + hop, shots))
+    pl.semaphore_wait(barrier, shots - 1 + jnp.where(has_up, 1, 0) + jnp.where(has_down, 1, 0))
 
     def remote(src, dst, send, recv, **to):
         return pltpu.make_async_remote_copy(
@@ -146,14 +126,14 @@
         )
 
     downs = (
-        (fields_in.at[:, 7:9, last], sig_near.at[0, :, 4:6, body, :]),
+        (sig.at[:, 4:6, last, body, :], sig_near.at[0, :, 4:6, body, :]),
         (fields_in.at[:, 3:7, last], sig_near.at[0, :, 0:4, body, :]),
         (fields_in.at[:, 7:9, last - 1], sig_far.at[:, 0:2]),
         (earth_in.at[:, last], mat_near.at[0]),
         (earth_in.at[2, last - 1], mat_far.at[0]),
     )
     ups = (
-        (fields_in.at[:, 5:6, 0], sig_near.at[1, :, 2:3, body, :]),
+        (sig.at[:, 2:3, 0, body, :], sig_near.at[1, :, 2:3, body, :]),
         (fields_in.at[:, 3:5, 0], sig_near.at[1, :, 0:2, body, :]),
         (fields_in.at[:, 6:9, 0], sig_near.at[1, :, 3:6, body, :]),
         (fields_in.at[:, 5, 1], sig_far.at[:, 2]),
@@ -168,8 +148,40 @@
         remote(src, dst, first_send.at[1, i], first_recv.at[1, i], gz=here - 1)
         for i, (src, dst) in enumerate(ups)
     ]
-    up_to(has_down, lambda: [copy.start() for copy in first_down])
-    up_to(has_up, lambda: [copy.start() for copy in first_up])
+    loads[0].wait()
+    up_to(has_down, first_down[0].start)
+    up_to(has_up, first_up[0].start)
+    up_to(has_down, lambda: [copy.start() for copy in first_down[1:]])
+    up_to(has_up, lambda: [copy.start() for copy in first_up[1:]])
+
+    zeros = jnp.zeros((GUARD, cols), jnp.float32)
+
+    def clear_around(ref, *extents):
+        for index in itertools.product(*[range(extent) for extent in extents]):
+            ref[(*index, pl.ds(0, GUARD), slice(None))] = zeros
+            ref[(*index, pl.ds(GUARD + rows, GUARD), slice(None))] = zeros
+
+    clear_around(sig, 2, 6, depth)
+    clear_around(vel, 2, 2, 3, depth)
+    clear_around(vel_near, 2, 2, 3)
+    clear_around(vel_msg, 2, 2, 2, 3, 2)
+    clear_around(vel_mid, steps // 2 - 1, 2, 2, 3)
+    clear_around(sig_near, 2, 2, 6)
+
+    def outside(side):
+        far = pl.ds(0, 2) if side == 0 else pl.ds(2, 1)
+        for view in (
+            vel_msg.at[:, side, :, :, :, body, :],
+            vel_mid.at[:, side, :, :, body, :],
+            sig_near.at[side, :, :, body, :],
+            sig_far.at[:, far],
+            mat_near.at[side],
+            mat_far.at[pl.ds(side, 1 + side)],
+        ):
+            view[...] = jnp.zeros(view.shape, jnp.float32)
+
+    up_to(here == 0, lambda: outside(0))
+    up_to(here == slabs - 1, lambda: outside(1))
 
     def message(w, slot, side):
         planes = pl.ds(depth - 2, 2) if side == 0 else pl.ds(0, 2)
@@ -203,17 +215,31 @@
     cells = (depth + 2) * rows
     receiver_row = (receiver_depth[...] - here * depth + 1) * rows + receiver_column[...] // cols
     receiver_col = receiver_column[...] % cols
-    in_row = lax.broadcasted_iota(jnp.int32, (cells, receivers), 0) == receiver_row
-    in_col = lax.broadcasted_iota(jnp.int32, (cols, receivers), 0) == receiver_col
-    in_col = jnp.where(in_col, 1.0, 0.0)
+    twice_row = jnp.concatenate([receiver_row, receiver_row], axis=1)
+    twice_col = jnp.concatenate([receiver_col, receiver_col], axis=1)
+    in_row = lax.broadcasted_iota(jnp.int32, (cells, 2 * receivers), 0) == twice_row
+    in_col = lax.broadcasted_iota(jnp.int32, (cols, 2 * receivers), 0) == twice_col
+    in_col = jnp.where(in_col, 1.0, 0.0).astype(jnp.bfloat16)
+    in_col = jnp.concatenate([in_col, in_col], axis=1)
+
+    def in_bf16(f):
+        return f.astype(jnp.bfloat16).astype(jnp.float32)
+
+    amounts = time_step * traces[0]
+    high = in_bf16(amounts)
+    middle_part = in_bf16(amounts - high)
+    low = in_bf16((amounts - high) - middle_part)
+    parts[0] = jnp.concatenate([high, middle_part], axis=1)
+    parts[1] = jnp.concatenate([low, jnp.zeros_like(low)], axis=1)
 
     def receivers_at(n, carry):
-        amount = jnp.where(in_row, time_step * traces[0, pl.ds(n, 1), :], 0.0)
+        spread = [
+            jnp.where(in_row, parts[i, pl.ds(n, 1), :], 0.0).astype(jnp.bfloat16) for i in range(2)
+        ]
         inject[n] = lax.dot_general(
-            amount,
+            jnp.concatenate(spread, axis=1),
             in_col,
             (((1,), (1,)), ((), ())),
-            precision=lax.Precision.HIGHEST,
             preferred_element_type=jnp.float32,
         ).reshape(depth + 2, rows, cols)
         return carry
@@ -221,7 +247,7 @@
     lax.fori_loop(0, steps, receivers_at, 0)
     image[...] = jnp.zeros_like(image)
 
-    for copy in loads:
+    for copy in loads[1:]:
         copy.wait()
     mat[...] = time_step * mat[...]
 
@@ -259,22 +285,29 @@
             return mat_near[0 if e < 0 else 1, which]
         return mat_far[0 if e < 0 else which]
 
-    def velocity(w, e, n, old, slot):
-        sxx, syy, szz, sxy, sxz, syz = [s(w, f, e) for f in range(6)]
-        fx = (s(w, SXX, e, after) - sxx) + b_y(sxy) + (sxz - s(w, SXZ, e - 1))
-        fy = (sxy - s(w, SXY, e, before)) + f_y(syy) + (syz - s(w, SYZ, e - 1))
-        fz = (sxz - s(w, SXZ, e, before)) + b_y(syz) + (s(w, SZZ, e + 1) - szz)
+    def velocity(w, e, n, old, slot, parts_of=(0, 1, 2)):
+        sxz, syz = s(w, SXZ, e), s(w, SYZ, e)
+        if 0 in parts_of or 1 in parts_of:
+            sxx, syy, sxy = s(w, SXX, e), s(w, SYY, e), s(w, SXY, e)
+        forces = {}
+        if 0 in parts_of:
+            forces[0] = (s(w, SXX, e, after) - sxx) + b_y(sxy) + (sxz - s(w, SXZ, e - 1))
+        if 1 in parts_of:
+            forces[1] = (sxy - s(w, SXY, e, before)) + f_y(syy) + (syz - s(w, SYZ, e - 1))
+        if 2 in parts_of:
+            up = s(w, SZZ, e + 1) - s(w, SZZ, e)
+            forces[2] = (sxz - s(w, SXZ, e, before)) + b_y(syz) + up
         buoyancy = m(0, e)
-        moved = [v(old, slot, w, c, e) + buoyancy * f for c, f in enumerate((fx, fy, fz))]
-        if w == 1:
-            moved[2] = moved[2] + inject[n, e + 1]
-        for c in range(3):
+        for c, force in forces.items():
+            moved = v(old, slot, w, c, e) + buoyancy * force
+            if c == 2 and w == 1:
+                moved = moved + inject[n, e + 1]
             if 0 <= e < depth:
-                vel[1 - old, w, c, e, body, :] = moved[c]
+                vel[1 - old, w, c, e, body, :] = moved
             else:
-                vel_near[0 if e < 0 else 1, w, c, body, :] = moved[c]
-
-    def normal(parity, slot, w, e, n, spun=None):
+                vel_near[0 if e < 0 else 1, w, c, body, :] = moved
+
+    def normal(parity, slot, w, e, n, spun=None, z_only=False):
         vx, vy, vz = [v(parity, slot, w, c, e) for c in range(3)]
         ex = vx - v(parity, slot, w, 0, e, before)
         ey = b_y(vy)
@@ -284,7 +317,7 @@
         if w == 0:
             common = common + source_at[e + 1] * wavelet[0, n]
         szz = add_s(w, SZZ, e, common + twice * ez)
-        if e > depth:
+        if z_only:
             return
         sxx = add_s(w, SXX, e, common + twice * ex)
         syy = add_s(w, SYY, e, common + twice * ey)
@@ -356,9 +389,10 @@
         normal(0, slot, w, depth, n)
         shear_flat(0, slot, w, depth)
         shear_deep(0, slot, w, depth)
-        normal(0, slot, w, depth + 1, n)
+        if not final:
+            normal(0, slot, w, depth + 1, n, z_only=True)
         velocity(w, last, n + 1, 0, slot)
-        velocity(w, depth, n + 1, 0, slot)
+        velocity(w, depth, n + 1, 0, slot, (0, 1) if final else (0, 1, 2))
         normal(1, slot, w, last, n + 1)
         shear(1, slot, w, last - 1)
         shear(1, slot, w, last)
@@ -375,11 +409,12 @@
         up_to(comes[0], message(w, slot, 0).wait_recv)
         normal(0, slot, w, 0, n, spun=0)
         shear_deep(0, slot, w, -1)
-        shear_flat(0, slot, w, -1)
-        normal(0, slot, w, -1, n)
-        shear_deep(0, slot, w, -2)
+        normal(0, slot, w, -1, n, z_only=final)
+        if not final:
+            shear_flat(0, slot, w, -1)
+            shear_deep(0, slot, w, -2)
         velocity(w, 0, n + 1, 0, slot)
-        velocity(w, -1, n + 1, 0, slot)
+        velocity(w, -1, n + 1, 0, slot, (2,) if final else (0, 1, 2))
         normal(1, slot, w, 0, n + 1)
         normal(1, slot, w, 1, n + 1, spun=1)
         shear(1, slot, w, 0)
@@ -396,7 +431,7 @@
         for w in range(2):
             up_to(comes[1], middle(w, cycle, 1).wait_recv)
             shear_deep(1, cycle, w, depth)
-            normal(1, cycle, w, depth + 1, n)
+            normal(1, cycle, w, depth + 1, n, z_only=True)
             up_to(comes[0], middle(w, cycle, 0).wait_recv)
             normal(1, cycle, w, -1, n)
             shear_deep(1, cycle, w, -2)
@@ -417,6 +452,9 @@
     mat_near[...] = time_step * mat_near[...]
     mat_far[...] = time_step * mat_far[...]
 
+    up_to(has_down, first_down[0].wait_send)
+    up_to(has_up, first_up[0].wait_send)
+
     cycles = steps // 2
 
     def cycle_body(cycle, carry):
@@ -435,52 +473,41 @@
 
     lax.fori_loop(0, cycles - 1, cycle_body, 0)
 
-    def first_round(half, i):
+    def to_shot(half, hop, source):
         planes = pl.ds(2 * half, 2)
         return remote(
-            image.at[i, planes],
-            landed.at[0, i, planes],
-            sum_send.at[0, half, i],
-            sum_recv.at[0, half, i],
-            shot=partners[i],
+            image.at[:, planes],
+            out.at[source, :, planes],
+            sum_send.at[half, hop],
+            sum_recv.at[half, hop],
+            shot=lax.rem(shot + hop, shots),
         )
 
-    def second_round(half, i):
+    def keep(half):
         planes = pl.ds(2 * half, 2)
-        return remote(
-            partial.at[i, planes],
-            landed.at[1, i, planes],
-            sum_send.at[1, half, i],
-            sum_recv.at[1, half, i],
-            shot=partners[1 - i],
-        )
+        return pltpu.make_async_copy(image.at[:, planes], out.at[shot, :, planes], keep_sem.at[half])
+
+    def hand_over(half):
+        for hop in (2, 1, 3):
+            to_shot(half, hop, shot).start()
+        keep(half).start()
 
     end = (cycles - 1) % 2
     for w in range(2):
         lower(end, w, steps - 2, True)
-    for i in range(2):
-        first_round(1, i).start()
+    hand_over(1)
     for w in range(2):
         upper(end, w, steps - 2, True)
-    for i in range(2):
-        first_round(0, i).start()
+    hand_over(0)
+    up_to(has_down, lambda: [copy.wait_send() for copy in first_down[1:]])
+    up_to(has_up, lambda: [copy.wait_send() for copy in first_up[1:]])
     for half in (1, 0):
-        planes = pl.ds(2 * half, 2)
-        for i in range(2):
-            first_round(half, i).wait_recv()
-            partial[i, planes] = image[i, planes] + landed[0, i, planes]
-            second_round(half, i).start()
+        keep(half).wait()
+        for hop in others:
+            to_shot(half, hop, lax.rem(shot + shots - hop, shots)).wait_recv()
     for half in (1, 0):
-        planes = pl.ds(2 * half, 2)
-        for i in range(2):
-            second_round(half, i).wait_recv()
-            out[i, planes] = partial[i, planes] + landed[1, i, planes]
-    for half in (1, 0):
-        for i in range(2):
-            first_round(half, i).wait_send()
-            second_round(half, i).wait_send()
-    up_to(has_down, lambda: [copy.wait_send() for copy in first_down])
-    up_to(has_up, lambda: [copy.wait_send() for copy in first_up])
+        for hop in others:
+            to_shot(half, hop, shot).wait_send()
 
 
 def solution(mesh):
@@ -495,13 +522,12 @@
         f32 = jnp.float32
         mids = steps // 2 - 1
         hbm = pl.BlockSpec(memory_space=pltpu.HBM)
-        vmem = pl.BlockSpec(memory_space=pltpu.VMEM)
         dma = pltpu.SemaphoreType.DMA
-        summed = pl.pallas_call(
+        by_shot = pl.pallas_call(
             functools.partial(window_kernel, dims),
-            out_shape=jax.ShapeDtypeStruct((2, depth, rows, cols), f32),
+            out_shape=jax.ShapeDtypeStruct((shots, 2, depth, rows, cols), f32),
             in_specs=[hbm] * 8,
-            out_specs=vmem,
+            out_specs=hbm,
             scratch_shapes=[
                 pltpu.VMEM((2, 2, 3, depth, padded, cols), f32),
                 pltpu.VMEM((2, 2, 2, 3, 2, padded, cols), f32),
@@ -518,8 +544,7 @@
                 pltpu.VMEM((2, depth, rows, cols), f32),
                 pltpu.VMEM((2, rows, cols), f32),
                 pltpu.VMEM((2, depth, rows, cols), f32),
-                pltpu.VMEM((2, depth, rows, cols), f32),
-                pltpu.VMEM((2, 2, depth, rows, cols), f32),
+                pltpu.VMEM((2, steps, 2 * receivers), f32),
                 pltpu.SMEM(s_depth.shape, jnp.int32),
                 pltpu.SMEM(s_column.shape, jnp.int32),
                 pltpu.SMEM(wavelet.shape, f32),
@@ -528,18 +553,21 @@
                 pltpu.VMEM(traces.shape, f32),
                 dma((3,)),
                 dma((6,)),
+                dma((2,)),
                 dma((2, 6)),
                 dma((2, 6)),
                 dma((2, 2, 2)),
                 dma((2, 2, 2)),
                 dma((mids, 2, 2)),
                 dma((mids, 2, 2)),
-                dma((2, 2, 2)),
-                dma((2, 2, 2)),
+                dma((2, shots)),
+                dma((2, shots)),
             ],
-            compiler_params=pltpu.CompilerParams(collective_id=0, has_side_effects=True),
+            compiler_params=pltpu.CompilerParams(
+                collective_id=0, has_side_effects=True
+            ),
         )(wavefields[0], earth, s_depth, s_column, wavelet, r_depth, r_column, traces)
-        return summed / steps
+        return sum(by_shot[i] for i in range(1, shots)) / steps + by_shot[0] / steps
 
     sharded = P(("parts", "shot"))
     return jax.shard_map(

time: 50.2 us -> 48.4 us (0.964)
  Pallas kernels: 47.1 us -> 45.1 us
    pallas_call x1, Pallas kernels: 47.1 us -> 45.1 us  [on_device(): pl.pallas_call(functools.partial(window_kernel, dims), out_shape=jax.Shap...]
    add x0 -> x1, other arithmetic: none -> 1.79 us  [on_device(): sum((by_shot[i] for i in range(1, shots))) / steps + by_shot[0] / steps]
    div x1 -> x0, other arithmetic: 1.57 us -> none  [on_device(): return summed / steps]
where the time goes in v3:
time: 48.4 us; the launch traced here: 48.2 us
  Pallas kernels  45.1 us (93%)
  other arithmetic  1.79 us (4%)
  between operations  1.3 us (3%)
    pallas_call x1, Pallas kernels, on_device(): pl.pallas_call(functools.partial(window_kernel, dims), out_shape=jax.Shap...  45.1 us
    add x1, other arithmetic, on_device(): sum((by_shot[i] for i in range(1, shots))) / steps + by_shot[0] / steps  1.79 us

profile of v3, /device:TPU:33, one launch (start us, length us, event | category | flops | bytes accessed | tf_op | source)
XLA Modules:
  0.0 48.2 jit_solution(10021345502106441309)
XLA Ops:
  1.3 45.1 %shard_map.82 = f32[4,2,4,32,128]{4,3,2,1,0:T(8,128)} custom-call(f32[2,9,4,32,128]{4,3,2,1,0:T(8,128)} %bitcast.3, f32[3,4,32,128]{3,2,1,0:T(8,128)} %earth_in.1, s32[1]{0:T(128)S(6)} %copy.9.source_depth_in, s32[1]{0:T(128)S(6)} %copy.10.source_column_in, f32[1,8]{1,0:T(1,128)} %wavelet_in.1, s32[1,64]{1,0:T(1,128)} %receiver_depth_in.1, ...), custom_call_target="tpu_custom_call" | custom-call | tf_op jit(solution)/shard_map/pallas_call | solution.py:526
  46.4 1.8 %multiply_bitcast_fusion = f32[2,4,32,128]{3,2,1,0:T(8,128)} fusion(f32[4,2,4,32,128]{4,3,2,1,0:T(8,128)} %shard_map.82), kind=kLoop, calls=%fused_computation | loop fusion | flops 131072 | bytes 655360 | tf_op jit(solution)/shard_map/add | solution.py:570

commit v4 on v3

--- a/solution.py
+++ b/solution.py
@@ -40,6 +40,8 @@
     press,
     spin,
     image,
+    partial,
+    landed,
     parts,
     source_depth,
     source_column,
@@ -115,10 +117,10 @@
 
     up_to(has_down, lambda: greet(gz=here + 1))
     up_to(has_up, lambda: greet(gz=here - 1))
-    others = range(1, shots)
-    for hop in others:
-        greet(shot=lax.rem(shot + hop, shots))
-    pl.semaphore_wait(barrier, shots - 1 + jnp.where(has_up, 1, 0) + jnp.where(has_down, 1, 0))
+    partners = (shot + 1 - 2 * lax.rem(shot, 2), shots - 1 - shot)
+    for partner in partners:
+        greet(shot=partner)
+    pl.semaphore_wait(barrier, 2 + jnp.where(has_up, 1, 0) + jnp.where(has_down, 1, 0))
 
     def remote(src, dst, send, recv, **to):
         return pltpu.make_async_remote_copy(
@@ -473,41 +475,60 @@
 
     lax.fori_loop(0, cycles - 1, cycle_body, 0)
 
-    def to_shot(half, hop, source):
-        planes = pl.ds(2 * half, 2)
+    pieces = ((2, 2), (0, 1), (1, 1))
+
+    def first_round(piece, i):
+        planes = pl.ds(*pieces[piece])
         return remote(
-            image.at[:, planes],
-            out.at[source, :, planes],
-            sum_send.at[half, hop],
-            sum_recv.at[half, hop],
-            shot=lax.rem(shot + hop, shots),
+            image.at[i, planes],
+            landed.at[i, planes],
+            sum_send.at[0, piece, i],
+            sum_recv.at[0, piece, i],
+            shot=partners[i],
         )
 
-    def keep(half):
-        planes = pl.ds(2 * half, 2)
-        return pltpu.make_async_copy(image.at[:, planes], out.at[shot, :, planes], keep_sem.at[half])
-
-    def hand_over(half):
-        for hop in (2, 1, 3):
-            to_shot(half, hop, shot).start()
-        keep(half).start()
+    def second_round(piece, i):
+        planes = pl.ds(*pieces[piece])
+        return remote(
+            partial.at[i, planes],
+            out.at[1, i, planes],
+            sum_send.at[1, piece, i],
+            sum_recv.at[1, piece, i],
+            shot=partners[1 - i],
+        )
+
+    def keep(piece, i):
+        planes = pl.ds(*pieces[piece])
+        return pltpu.make_async_copy(partial.at[i, planes], out.at[0, i, planes], keep_sem.at[piece, i])
 
     end = (cycles - 1) % 2
     for w in range(2):
         lower(end, w, steps - 2, True)
-    hand_over(1)
+    for i in range(2):
+        first_round(0, i).start()
     for w in range(2):
         upper(end, w, steps - 2, True)
-    hand_over(0)
+    for piece in (1, 2):
+        for i in range(2):
+            first_round(piece, i).start()
+    for piece in range(3):
+        planes = pl.ds(*pieces[piece])
+        for i in range(2):
+            first_round(piece, i).wait_recv()
+            partial[i, planes] = image[i, planes] + landed[i, planes]
+        for i in range(2):
+            second_round(piece, i).start()
+            keep(piece, i).start()
     up_to(has_down, lambda: [copy.wait_send() for copy in first_down[1:]])
     up_to(has_up, lambda: [copy.wait_send() for copy in first_up[1:]])
-    for half in (1, 0):
-        keep(half).wait()
-        for hop in others:
-            to_shot(half, hop, lax.rem(shot + shots - hop, shots)).wait_recv()
-    for half in (1, 0):
-        for hop in others:
-            to_shot(half, hop, shot).wait_send()
+    for piece in range(3):
+        for i in range(2):
+            first_round(piece, i).wait_send()
+            keep(piece, i).wait()
+            second_round(piece, i).wait_send()
+    for piece in range(3):
+        for i in range(2):
+            second_round(piece, i).wait_recv()
 
 
 def solution(mesh):
@@ -523,9 +544,9 @@
         mids = steps // 2 - 1
         hbm = pl.BlockSpec(memory_space=pltpu.HBM)
         dma = pltpu.SemaphoreType.DMA
-        by_shot = pl.pallas_call(
+        pairs = pl.pallas_call(
             functools.partial(window_kernel, dims),
-            out_shape=jax.ShapeDtypeStruct((shots, 2, depth, rows, cols), f32),
+            out_shape=jax.ShapeDtypeStruct((2, 2, depth, rows, cols), f32),
             in_specs=[hbm] * 8,
             out_specs=hbm,
             scratch_shapes=[
@@ -544,6 +565,8 @@
                 pltpu.VMEM((2, depth, rows, cols), f32),
                 pltpu.VMEM((2, rows, cols), f32),
                 pltpu.VMEM((2, depth, rows, cols), f32),
+                pltpu.VMEM((2, depth, rows, cols), f32),
+                pltpu.VMEM((2, depth, rows, cols), f32),
                 pltpu.VMEM((2, steps, 2 * receivers), f32),
                 pltpu.SMEM(s_depth.shape, jnp.int32),
                 pltpu.SMEM(s_column.shape, jnp.int32),
@@ -553,21 +576,21 @@
                 pltpu.VMEM(traces.shape, f32),
                 dma((3,)),
                 dma((6,)),
-                dma((2,)),
+                dma((3, 2)),
                 dma((2, 6)),
                 dma((2, 6)),
                 dma((2, 2, 2)),
                 dma((2, 2, 2)),
                 dma((mids, 2, 2)),
                 dma((mids, 2, 2)),
-                dma((2, shots)),
-                dma((2, shots)),
+                dma((2, 3, 2)),
+                dma((2, 3, 2)),
             ],
             compiler_params=pltpu.CompilerParams(
                 collective_id=0, has_side_effects=True
             ),
         )(wavefields[0], earth, s_depth, s_column, wavelet, r_depth, r_column, traces)
-        return sum(by_shot[i] for i in range(1, shots)) / steps + by_shot[0] / steps
+        return (pairs[0] + pairs[1]) / steps
 
     sharded = P(("parts", "shot"))
     return jax.shard_map(

time: 48.4 us -> 49.9 us (1.031)
  Pallas kernels: 45.1 us -> 46.8 us
    add x1 -> x0, other arithmetic: 1.79 us -> none  [on_device(): sum((by_shot[i] for i in range(1, shots))) / steps + by_shot[0] / steps]
    pallas_call x1, Pallas kernels: 45.1 us -> 46.8 us  [on_device(): pl.pallas_call(functools.partial(window_kernel, dims), out_shape=jax.Shap...]
    div x0 -> x1, other arithmetic: none -> 1.64 us  [on_device(): return (pairs[0] + pairs[1]) / steps]
where the time goes in v4:
time: 49.9 us; the launch traced here: 49.7 us
  Pallas kernels  46.8 us (94%)
  other arithmetic  1.64 us (3%)
  between operations  1.3 us (3%)
    pallas_call x1, Pallas kernels, on_device(): pl.pallas_call(functools.partial(window_kernel, dims), out_shape=jax.Shap...  46.8 us
    div x1, other arithmetic, on_device(): return (pairs[0] + pairs[1]) / steps  1.64 us

profile of v4, /device:TPU:33, one launch (start us, length us, event | category | flops | bytes accessed | tf_op | source)
XLA Modules:
  0.0 49.7 jit_solution(3400304980768754632)
XLA Ops:
  1.3 46.8 %shard_map.82 = f32[2,2,4,32,128]{4,3,2,1,0:T(8,128)} custom-call(f32[2,9,4,32,128]{4,3,2,1,0:T(8,128)} %bitcast.3, f32[3,4,32,128]{3,2,1,0:T(8,128)} %earth_in.1, s32[1]{0:T(128)S(6)} %copy.9.source_depth_in, s32[1]{0:T(128)S(6)} %copy.10.source_column_in, f32[1,8]{1,0:T(1,128)} %wavelet_in.1, s32[1,64]{1,0:T(1,128)} %receiver_depth_in.1, ...), custom_call_target="tpu_custom_call" | custom-call | tf_op jit(solution)/shard_map/pallas_call | solution.py:547
  48.1 1.6 %multiply_bitcast_fusion = f32[2,4,32,128]{3,2,1,0:T(8,128)} fusion(f32[2,2,4,32,128]{4,3,2,1,0:T(8,128)} %shard_map.82), kind=kLoop, calls=%fused_computation | loop fusion | flops 65536 | bytes 393216 | tf_op jit(solution)/shard_map/div | solution.py:593

commit v5 on v3

--- a/solution.py
+++ b/solution.py
@@ -362,6 +362,11 @@
         add_s(w, SXZ, e, mu * ((v(parity, slot, w, 0, e + 1) - vx) + z_along_x))
         add_s(w, SYZ, e, mu * ((v(parity, slot, w, 1, e + 1) - vy) + f_y(vz)))
 
+    def send_middle(cycle):
+        for w in range(2):
+            for side in range(2):
+                up_to(goes[side], middle(w, cycle, side).start)
+
     def inside(cycle, n, send):
         for w in range(2):
             for e in range(1, depth):
@@ -371,19 +376,12 @@
                 shear(0, None, w, e)
             for e in (1, 2):
                 velocity(w, e, n + 1, 0, None)
-
-            def start(w=w):
-                for side in range(2):
-                    up_to(goes[side], middle(w, cycle, side).start)
-
-            if send is True:
-                start()
-            else:
-                up_to(send, start)
             normal(1, None, w, 2, n + 1)
             shear(1, None, w, 1, spun=1)
+        up_to(send, lambda: send_middle(cycle))
 
     def lower(slot, w, n, final):
+        up_to(goes[0], message(w, slot, 0).wait_send)
         up_to(comes[1], message(w, slot, 1).wait_recv)
         shear(0, slot, w, last)
         normal(0, slot, w, depth, n)
@@ -396,7 +394,6 @@
         normal(1, slot, w, last, n + 1)
         shear(1, slot, w, last - 1)
         shear(1, slot, w, last)
-        up_to(goes[0], message(w, slot, 0).wait_send)
         if final:
             return
         normal(1, slot, w, depth, n + 1)
@@ -405,34 +402,40 @@
         up_to(goes[0], message(w, 1 - slot, 0).start)
         shear_flat(1, slot, w, depth)
 
-    def upper(slot, w, n, final):
-        up_to(comes[0], message(w, slot, 0).wait_recv)
-        normal(0, slot, w, 0, n, spun=0)
-        shear_deep(0, slot, w, -1)
-        normal(0, slot, w, -1, n, z_only=final)
-        if not final:
-            shear_flat(0, slot, w, -1)
-            shear_deep(0, slot, w, -2)
-        velocity(w, 0, n + 1, 0, slot)
-        velocity(w, -1, n + 1, 0, slot, (2,) if final else (0, 1, 2))
-        normal(1, slot, w, 0, n + 1)
-        normal(1, slot, w, 1, n + 1, spun=1)
-        shear(1, slot, w, 0)
-        up_to(goes[1], message(w, slot, 1).wait_send)
+    def upper(slot, n, final):
+        for w in range(2):
+            up_to(goes[1], message(w, slot, 1).wait_send)
+            up_to(comes[0], message(w, slot, 0).wait_recv)
+        for w in range(2):
+            normal(0, slot, w, 0, n, spun=0)
+            shear_deep(0, slot, w, -1)
+            normal(0, slot, w, -1, n, z_only=final)
+            if not final:
+                shear_flat(0, slot, w, -1)
+                shear_deep(0, slot, w, -2)
+            velocity(w, 0, n + 1, 0, slot)
+            velocity(w, -1, n + 1, 0, slot, (2,) if final else (0, 1, 2))
+            normal(1, slot, w, 0, n + 1)
+            normal(1, slot, w, 1, n + 1, spun=1)
+            shear(1, slot, w, 0)
+            if not final:
+                shear_deep(1, slot, w, -1)
+                velocity(w, 0, n + 2, 1, slot)
+                velocity(w, 1, n + 2, 1, slot)
         if final:
             return
-        shear_deep(1, slot, w, -1)
-        velocity(w, 0, n + 2, 1, slot)
-        velocity(w, 1, n + 2, 1, slot)
-        up_to(goes[1], message(w, 1 - slot, 1).start)
-        shear_flat(1, slot, w, -1)
+        for w in range(2):
+            up_to(goes[1], message(w, 1 - slot, 1).start)
+        for w in range(2):
+            shear_flat(1, slot, w, -1)
 
     def catch_up(cycle, n):
         for w in range(2):
-            up_to(comes[1], middle(w, cycle, 1).wait_recv)
+            for side in range(2):
+                up_to(comes[side], middle(w, cycle, side).wait_recv)
+        for w in range(2):
             shear_deep(1, cycle, w, depth)
             normal(1, cycle, w, depth + 1, n, z_only=True)
-            up_to(comes[0], middle(w, cycle, 0).wait_recv)
             normal(1, cycle, w, -1, n)
             shear_deep(1, cycle, w, -2)
 
@@ -441,12 +444,26 @@
         velocity(w, last, 0, 1, None)
         velocity(w, last - 1, 0, 1, None)
         up_to(goes[0], message(w, 0, 0).start)
+    for w in range(2):
+        velocity(w, 1, 0, 1, None)
+        velocity(w, 0, 0, 1, None, (2,))
+        for e in range(1, depth):
+            normal(0, None, w, e, 0)
+        for e in range(1, last):
+            shear(0, None, w, e)
+        velocity(w, 2, 1, 0, None)
+        velocity(w, 1, 1, 0, None, (2,))
+        normal(1, None, w, 2, 1)
     up_to(comes[0], first_down[0].wait_recv)
     for w in range(2):
-        velocity(w, 0, 0, 1, None)
-        velocity(w, 1, 0, 1, None)
+        velocity(w, 0, 0, 1, None, (0, 1))
+    for w in range(2):
         up_to(goes[1], message(w, 0, 1).start)
-    inside(0, 0, True)
+    for w in range(2):
+        shear(0, None, w, 0, spun=0)
+        velocity(w, 1, 1, 0, None, (0, 1))
+        shear(1, None, w, 1, spun=1)
+    send_middle(0)
     up_to(comes[1], lambda: [copy.wait_recv() for copy in first_up[1:]])
     up_to(comes[0], lambda: [copy.wait_recv() for copy in first_down[1:]])
     mat_near[...] = time_step * mat_near[...]
@@ -462,8 +479,7 @@
         n = 2 * cycle
         for w in range(2):
             lower(slot, w, n, False)
-        for w in range(2):
-            upper(slot, w, n, False)
+        upper(slot, n, False)
         for w in range(2):
             for side in range(2):
                 up_to(goes[side], middle(w, cycle, side).wait_send)
@@ -496,8 +512,7 @@
     for w in range(2):
         lower(end, w, steps - 2, True)
     hand_over(1)
-    for w in range(2):
-        upper(end, w, steps - 2, True)
+    upper(end, steps - 2, True)
     hand_over(0)
     up_to(has_down, lambda: [copy.wait_send() for copy in first_down[1:]])
     up_to(has_up, lambda: [copy.wait_send() for copy in first_up[1:]])

time: 48.4 us -> 49.6 us (1.025)
  Pallas kernels: 45.1 us -> 46.3 us
    pallas_call x1, Pallas kernels: 45.1 us -> 46.3 us  [on_device(): pl.pallas_call(functools.partial(window_kernel, dims), out_shape=jax.Shap...]
where the time goes in v5:
time: 49.6 us; the launch traced here: 49.4 us
  Pallas kernels  46.3 us (93%)
  other arithmetic  1.79 us (4%)
  between operations  1.3 us (3%)
    pallas_call x1, Pallas kernels, on_device(): pl.pallas_call(functools.partial(window_kernel, dims), out_shape=jax.Shap...  46.3 us
    add x1, other arithmetic, on_device(): sum((by_shot[i] for i in range(1, shots))) / steps + by_shot[0] / steps  1.79 us

profile of v5, /device:TPU:33, one launch (start us, length us, event | category | flops | bytes accessed | tf_op | source)
XLA Modules:
  0.0 49.4 jit_solution(4444884086053172557)
XLA Ops:
  1.3 46.3 %shard_map.82 = f32[4,2,4,32,128]{4,3,2,1,0:T(8,128)} custom-call(f32[2,9,4,32,128]{4,3,2,1,0:T(8,128)} %bitcast.3, f32[3,4,32,128]{3,2,1,0:T(8,128)} %earth_in.1, s32[1]{0:T(128)S(6)} %copy.9.source_depth_in, s32[1]{0:T(128)S(6)} %copy.10.source_column_in, f32[1,8]{1,0:T(1,128)} %wavelet_in.1, s32[1,64]{1,0:T(1,128)} %receiver_depth_in.1, ...), custom_call_target="tpu_custom_call" | custom-call | tf_op jit(solution)/shard_map/pallas_call | solution.py:541
  47.6 1.8 %multiply_bitcast_fusion = f32[2,4,32,128]{3,2,1,0:T(8,128)} fusion(f32[4,2,4,32,128]{4,3,2,1,0:T(8,128)} %shard_map.82), kind=kLoop, calls=%fused_computation | loop fusion | flops 131072 | bytes 655360 | tf_op jit(solution)/shard_map/add | solution.py:585

commit v6 on v3

--- a/solution.py
+++ b/solution.py
@@ -50,6 +50,9 @@
     load_sem,
     small_sem,
     keep_sem,
+    near_sem,
+    peers_sem,
+    ready_sem,
     first_send,
     first_recv,
     msg_send,
@@ -113,12 +116,24 @@
     def greet(**to):
         pl.semaphore_signal(barrier, inc=1, device_id=to, device_id_type=MESH)
 
-    up_to(has_down, lambda: greet(gz=here + 1))
-    up_to(has_up, lambda: greet(gz=here - 1))
     others = range(1, shots)
-    for hop in others:
-        greet(shot=lax.rem(shot + hop, shots))
-    pl.semaphore_wait(barrier, shots - 1 + jnp.where(has_up, 1, 0) + jnp.where(has_down, 1, 0))
+    odd = lax.rem(here, 2) == 1
+    even = lax.rem(here, 2) == 0
+
+    def greet_all():
+        greet(gz=here - 1)
+        up_to(has_down, lambda: greet(gz=here + 1))
+        for hop in others:
+            greet(shot=lax.rem(shot + hop, shots))
+
+    def answer(side, **to):
+        pl.semaphore_signal(near_sem.at[side], inc=1, device_id=to, device_id_type=MESH)
+
+    up_to(odd, greet_all)
+    beside = jnp.where(has_up, 1, 0) + jnp.where(has_down, 1, 0)
+    pl.semaphore_wait(barrier, jnp.where(even, beside, shots - 1))
+    up_to(even & has_down, lambda: answer(0, gz=here + 1))
+    up_to(even & has_up, lambda: answer(1, gz=here - 1))
 
     def remote(src, dst, send, recv, **to):
         return pltpu.make_async_remote_copy(
@@ -149,10 +164,11 @@
         for i, (src, dst) in enumerate(ups)
     ]
     loads[0].wait()
+    up_to(odd & has_down, lambda: pl.semaphore_wait(near_sem.at[1], 1))
     up_to(has_down, first_down[0].start)
-    up_to(has_up, first_up[0].start)
+    up_to(even & has_up, first_up[0].start)
     up_to(has_down, lambda: [copy.start() for copy in first_down[1:]])
-    up_to(has_up, lambda: [copy.start() for copy in first_up[1:]])
+    up_to(even & has_up, lambda: [copy.start() for copy in first_up[1:]])
 
     zeros = jnp.zeros((GUARD, cols), jnp.float32)
 
@@ -362,6 +378,11 @@
         add_s(w, SXZ, e, mu * ((v(parity, slot, w, 0, e + 1) - vx) + z_along_x))
         add_s(w, SYZ, e, mu * ((v(parity, slot, w, 1, e + 1) - vy) + f_y(vz)))
 
+    def send_middle(cycle):
+        for w in range(2):
+            for side in range(2):
+                up_to(goes[side], middle(w, cycle, side).start)
+
     def inside(cycle, n, send):
         for w in range(2):
             for e in range(1, depth):
@@ -371,19 +392,12 @@
                 shear(0, None, w, e)
             for e in (1, 2):
                 velocity(w, e, n + 1, 0, None)
-
-            def start(w=w):
-                for side in range(2):
-                    up_to(goes[side], middle(w, cycle, side).start)
-
-            if send is True:
-                start()
-            else:
-                up_to(send, start)
             normal(1, None, w, 2, n + 1)
             shear(1, None, w, 1, spun=1)
+        up_to(send, lambda: send_middle(cycle))
 
     def lower(slot, w, n, final):
+        up_to(goes[0], message(w, slot, 0).wait_send)
         up_to(comes[1], message(w, slot, 1).wait_recv)
         shear(0, slot, w, last)
         normal(0, slot, w, depth, n)
@@ -396,7 +410,6 @@
         normal(1, slot, w, last, n + 1)
         shear(1, slot, w, last - 1)
         shear(1, slot, w, last)
-        up_to(goes[0], message(w, slot, 0).wait_send)
         if final:
             return
         normal(1, slot, w, depth, n + 1)
@@ -429,10 +442,11 @@
 
     def catch_up(cycle, n):
         for w in range(2):
-            up_to(comes[1], middle(w, cycle, 1).wait_recv)
+            for side in range(2):
+                up_to(comes[side], middle(w, cycle, side).wait_recv)
+        for w in range(2):
             shear_deep(1, cycle, w, depth)
             normal(1, cycle, w, depth + 1, n, z_only=True)
-            up_to(comes[0], middle(w, cycle, 0).wait_recv)
             normal(1, cycle, w, -1, n)
             shear_deep(1, cycle, w, -2)
 
@@ -441,12 +455,36 @@
         velocity(w, last, 0, 1, None)
         velocity(w, last - 1, 0, 1, None)
         up_to(goes[0], message(w, 0, 0).start)
+    for w in range(2):
+        velocity(w, 1, 0, 1, None)
+        velocity(w, 0, 0, 1, None, (2,))
+        for e in range(1, depth):
+            normal(0, None, w, e, 0)
+        for e in range(1, last):
+            shear(0, None, w, e)
+        velocity(w, 2, 1, 0, None)
+        velocity(w, 1, 1, 0, None, (2,))
+        normal(1, None, w, 2, 1)
+
+    def upper_side_is_there():
+        pl.semaphore_wait(near_sem.at[0], 1)
+        for copy in first_up:
+            copy.start()
+        for hop in others:
+            to = {"shot": lax.rem(shot + hop, shots)}
+            pl.semaphore_signal(peers_sem, inc=1, device_id=to, device_id_type=MESH)
+
+    up_to(odd, upper_side_is_there)
     up_to(comes[0], first_down[0].wait_recv)
     for w in range(2):
-        velocity(w, 0, 0, 1, None)
-        velocity(w, 1, 0, 1, None)
+        velocity(w, 0, 0, 1, None, (0, 1))
+    for w in range(2):
         up_to(goes[1], message(w, 0, 1).start)
-    inside(0, 0, True)
+    for w in range(2):
+        shear(0, None, w, 0, spun=0)
+        velocity(w, 1, 1, 0, None, (0, 1))
+        shear(1, None, w, 1, spun=1)
+    send_middle(0)
     up_to(comes[1], lambda: [copy.wait_recv() for copy in first_up[1:]])
     up_to(comes[0], lambda: [copy.wait_recv() for copy in first_down[1:]])
     mat_near[...] = time_step * mat_near[...]
@@ -492,9 +530,15 @@
             to_shot(half, hop, shot).start()
         keep(half).start()
 
+    def pass_on():
+        pl.semaphore_wait(peers_sem, shots - 1)
+        pl.semaphore_signal(ready_sem, inc=1, device_id={"gz": here - 1}, device_id_type=MESH)
+
+    up_to(odd, pass_on)
     end = (cycles - 1) % 2
     for w in range(2):
         lower(end, w, steps - 2, True)
+    up_to(even, lambda: pl.semaphore_wait(ready_sem, 1))
     hand_over(1)
     for w in range(2):
         upper(end, w, steps - 2, True)
@@ -516,7 +560,7 @@
     def on_device(wavefields, earth, s_depth, s_column, wavelet, r_depth, r_column, traces):
         depth, rows, cols = earth.shape[1:]
         steps, receivers = traces.shape[1:]
-        assert depth == 4 and shots == 4 and steps % 2 == 0 and steps >= 4
+        assert depth == 4 and shots == 4 and slabs % 2 == 0 and steps % 2 == 0 and steps >= 4
         dims = (slabs, shots, depth, rows, cols, steps, receivers)
         padded = rows + 2 * GUARD
         f32 = jnp.float32
@@ -554,6 +598,9 @@
                 dma((3,)),
                 dma((6,)),
                 dma((2,)),
+                pltpu.SemaphoreType.REGULAR((2,)),
+                pltpu.SemaphoreType.REGULAR,
+                pltpu.SemaphoreType.REGULAR,
                 dma((2, 6)),
                 dma((2, 6)),
                 dma((2, 2, 2)),

time: 48.4 us -> 45.2 us (0.934)
  Pallas kernels: 45.1 us -> 42 us
    pallas_call x1, Pallas kernels: 45.1 us -> 42 us  [on_device(): pl.pallas_call(functools.partial(window_kernel, dims), out_shape=jax.Shap...]
where the time goes in v6:
time: 45.2 us; the launch traced here: 45.1 us
  Pallas kernels  42 us (93%)
  other arithmetic  1.79 us (4%)
  between operations  1.3 us (3%)
    pallas_call x1, Pallas kernels, on_device(): pl.pallas_call(functools.partial(window_kernel, dims), out_shape=jax.Shap...  42 us
    add x1, other arithmetic, on_device(): sum((by_shot[i] for i in range(1, shots))) / steps + by_shot[0] / steps  1.79 us

profile of v6, /device:TPU:33, one launch (start us, length us, event | category | flops | bytes accessed | tf_op | source)
XLA Modules:
  0.0 45.1 jit_solution(7485513725128743118)
XLA Ops:
  1.3 42.0 %shard_map.82 = f32[4,2,4,32,128]{4,3,2,1,0:T(8,128)} custom-call(f32[2,9,4,32,128]{4,3,2,1,0:T(8,128)} %bitcast.3, f32[3,4,32,128]{3,2,1,0:T(8,128)} %earth_in.1, s32[1]{0:T(128)S(6)} %copy.9.source_depth_in, s32[1]{0:T(128)S(6)} %copy.10.source_column_in, f32[1,8]{1,0:T(1,128)} %wavelet_in.1, s32[1,64]{1,0:T(1,128)} %receiver_depth_in.1, ...), custom_call_target="tpu_custom_call" | custom-call | tf_op jit(solution)/shard_map/pallas_call | solution.py:570
  43.3 1.8 %multiply_bitcast_fusion = f32[2,4,32,128]{3,2,1,0:T(8,128)} fusion(f32[4,2,4,32,128]{4,3,2,1,0:T(8,128)} %shard_map.82), kind=kLoop, calls=%fused_computation | loop fusion | flops 131072 | bytes 655360 | tf_op jit(solution)/shard_map/add | solution.py:617

commit v7 on v6

--- a/solution.py
+++ b/solution.py
@@ -537,12 +537,12 @@
     up_to(odd, pass_on)
     end = (cycles - 1) % 2
     for w in range(2):
+        upper(end, w, steps - 2, True)
+    up_to(even, lambda: pl.semaphore_wait(ready_sem, 1))
+    hand_over(0)
+    for w in range(2):
         lower(end, w, steps - 2, True)
-    up_to(even, lambda: pl.semaphore_wait(ready_sem, 1))
     hand_over(1)
-    for w in range(2):
-        upper(end, w, steps - 2, True)
-    hand_over(0)
     up_to(has_down, lambda: [copy.wait_send() for copy in first_down[1:]])
     up_to(has_up, lambda: [copy.wait_send() for copy in first_up[1:]])
     for half in (1, 0):

time: 45.2 us -> 44.6 us (0.987)
  Pallas kernels: 42 us -> 41.2 us
    pallas_call x1, Pallas kernels: 42 us -> 41.2 us  [on_device(): pl.pallas_call(functools.partial(window_kernel, dims), out_shape=jax.Shap...]
where the time goes in v7:
time: 44.6 us; the launch traced here: 44.2 us
  Pallas kernels  41.2 us (92%)
  other arithmetic  1.79 us (4%)
  between operations  1.3 us (3%)
    pallas_call x1, Pallas kernels, on_device(): pl.pallas_call(functools.partial(window_kernel, dims), out_shape=jax.Shap...  41.2 us
    add x1, other arithmetic, on_device(): sum((by_shot[i] for i in range(1, shots))) / steps + by_shot[0] / steps  1.79 us

profile of v7, /device:TPU:33, one launch (start us, length us, event | category | flops | bytes accessed | tf_op | source)
XLA Modules:
  0.0 44.2 jit_solution(14680655250816352286)
XLA Ops:
  1.3 41.2 %shard_map.82 = f32[4,2,4,32,128]{4,3,2,1,0:T(8,128)} custom-call(f32[2,9,4,32,128]{4,3,2,1,0:T(8,128)} %bitcast.3, f32[3,4,32,128]{3,2,1,0:T(8,128)} %earth_in.1, s32[1]{0:T(128)S(6)} %copy.9.source_depth_in, s32[1]{0:T(128)S(6)} %copy.10.source_column_in, f32[1,8]{1,0:T(1,128)} %wavelet_in.1, s32[1,64]{1,0:T(1,128)} %receiver_depth_in.1, ...), custom_call_target="tpu_custom_call" | custom-call | tf_op jit(solution)/shard_map/pallas_call | solution.py:570
  42.5 1.8 %multiply_bitcast_fusion = f32[2,4,32,128]{3,2,1,0:T(8,128)} fusion(f32[4,2,4,32,128]{4,3,2,1,0:T(8,128)} %shard_map.82), kind=kLoop, calls=%fused_computation | loop fusion | flops 131072 | bytes 655360 | tf_op jit(solution)/shard_map/add | solution.py:617

commit v8 on v7

--- a/solution.py
+++ b/solution.py
@@ -82,13 +82,17 @@
         return jnp.where(at_last, 0.0, pltpu.roll(f, cols - 1, 1)) - f
 
     loads = [
-        pltpu.make_async_copy(
-            fields_in.at[:, 3:9], sig.at[:, :, :, body, :], load_sem.at[0]
-        ),
-        pltpu.make_async_copy(
-            fields_in.at[:, 0:3], vel.at[1, :, :, :, body, :], load_sem.at[1]
-        ),
-        pltpu.make_async_copy(earth_in, mat, load_sem.at[2]),
+        pltpu.make_async_copy(src, dst, load_sem.at[i])
+        for i, (src, dst) in enumerate(
+            (
+                (fields_in.at[:, 7:9], sig.at[:, 4:6, :, body, :]),
+                (fields_in.at[:, 5:6], sig.at[:, 2:3, :, body, :]),
+                (fields_in.at[:, 3:5], sig.at[:, 0:2, :, body, :]),
+                (fields_in.at[:, 6:7], sig.at[:, 3:4, :, body, :]),
+                (fields_in.at[:, 0:3], vel.at[1, :, :, :, body, :]),
+                (earth_in, mat),
+            )
+        )
     ]
     small = [
         pltpu.make_async_copy(src, dst, small_sem.at[i])
@@ -164,6 +168,7 @@
         for i, (src, dst) in enumerate(ups)
     ]
     loads[0].wait()
+    loads[1].wait()
     up_to(odd & has_down, lambda: pl.semaphore_wait(near_sem.at[1], 1))
     up_to(has_down, first_down[0].start)
     up_to(even & has_up, first_up[0].start)
@@ -263,7 +268,7 @@
     lax.fori_loop(0, steps, receivers_at, 0)
     image[...] = jnp.zeros_like(image)
 
-    for copy in loads[1:]:
+    for copy in loads[2:]:
         copy.wait()
     mat[...] = time_step * mat[...]
 
@@ -526,7 +531,7 @@
         return pltpu.make_async_copy(image.at[:, planes], out.at[shot, :, planes], keep_sem.at[half])
 
     def hand_over(half):
-        for hop in (2, 1, 3):
+        for hop in (1, 2, 3):
             to_shot(half, hop, shot).start()
         keep(half).start()
 
@@ -595,7 +600,7 @@
                 pltpu.VMEM(r_depth.shape, jnp.int32),
                 pltpu.VMEM(r_column.shape, jnp.int32),
                 pltpu.VMEM(traces.shape, f32),
-                dma((3,)),
+                dma((6,)),
                 dma((6,)),
                 dma((2,)),
                 pltpu.SemaphoreType.REGULAR((2,)),

time: 44.6 us -> 44.3 us (level)
  no operation moved by 1% of the time
where the time goes in v8:
time: 44.3 us; the launch traced here: 44.1 us
  Pallas kernels  41 us (93%)
  other arithmetic  1.79 us (4%)
  between operations  1.3 us (3%)
    pallas_call x1, Pallas kernels, on_device(): pl.pallas_call(functools.partial(window_kernel, dims), out_shape=jax.Shap...  41 us
    add x1, other arithmetic, on_device(): sum((by_shot[i] for i in range(1, shots))) / steps + by_shot[0] / steps  1.79 us

profile of v8, /device:TPU:33, one launch (start us, length us, event | category | flops | bytes accessed | tf_op | source)
XLA Modules:
  0.0 44.1 jit_solution(9097916388814465412)
XLA Ops:
  1.3 41.0 %shard_map.82 = f32[4,2,4,32,128]{4,3,2,1,0:T(8,128)} custom-call(f32[2,9,4,32,128]{4,3,2,1,0:T(8,128)} %bitcast.3, f32[3,4,32,128]{3,2,1,0:T(8,128)} %earth_in.1, s32[1]{0:T(128)S(6)} %copy.9.source_depth_in, s32[1]{0:T(128)S(6)} %copy.10.source_column_in, f32[1,8]{1,0:T(1,128)} %wavelet_in.1, s32[1,64]{1,0:T(1,128)} %receiver_depth_in.1, ...), custom_call_target="tpu_custom_call" | custom-call | tf_op jit(solution)/shard_map/pallas_call | solution.py:575
  42.3 1.8 %multiply_bitcast_fusion = f32[2,4,32,128]{3,2,1,0:T(8,128)} fusion(f32[4,2,4,32,128]{4,3,2,1,0:T(8,128)} %shard_map.82), kind=kLoop, calls=%fused_computation | loop fusion | flops 131072 | bytes 655360 | tf_op jit(solution)/shard_map/add | solution.py:622
